TPU v7x, 32 devices: a whole 2x2x4 slice. The times are simulated.
32 devices in a mesh: gx: 2 (over x), gy: 4 (over z), band: 4 (over y, core).
Axes of the slice: x: 2, y: 2, z: 4, core: 2. Of those that a mesh axis runs over, the one named last changes fastest.
Arguments:
- orbitals: float32 [2, 16, 16, 48, 128], P(None, 'band', 'gx', 'gy'), may hold values from -3 to 3
- external: float32 [16, 48, 128], P('gx', 'gy'), may hold values from 2 to 6
Outputs:
- orbitals_next: float32 [2, 16, 16, 48, 128], P(None, 'band', 'gx', 'gy')
- potential_next: float32 [16, 48, 128], P('gx', 'gy')
All inputs are finite; a program needn't handle non-finite values.
Results may differ from a plain program's by a relative error of at most 0.00002.
Values sent between devices are 32-bit elements; how exact they have to be, the bound alone decides.
A program may use at most 64 MiB of HBM per device.

v0:
```python
import functools

import jax
import jax.numpy as jnp
from jax import lax
from jax.experimental import pallas as pl
from jax.experimental.pallas import tpu as pltpu
from jax.sharding import PartitionSpec as P

step_length = 0.15
exchange_coef = 0.7386
centre_weight = -2.5
near_weight = 4.0 / 3.0
far_weight = -1.0 / 12.0
MESH = pl.DeviceIdType.MESH


def cube_root(d):
    guess = jnp.exp(jnp.log(d) * (1.0 / 3.0))
    better = guess - (guess - d / (guess * guess)) * (1.0 / 3.0)
    return jnp.where(d > 1e-30, better, guess)


def kernel(counts, orb_hbm, ext_hbm, out_ref, pot_ref, *scratch):
    terms = scratch[:8]
    orb_ref, ext_ref, pot_wide, density, in_sem, x_send, x_recv, y_send, y_recv, d_send, d_recv = scratch[8:]
    n_x, n_y, n_b = counts
    nf, ny, nx, nz = orb_ref.shape
    gx = lax.axis_index("gx")
    gy = lax.axis_index("gy")
    gb = lax.axis_index("band")
    has = {
        ("gx", 0): gx > 0,
        ("gx", 1): gx < n_x - 1,
        ("gy", 0): gy > 0,
        ("gy", 1): gy < n_y - 1,
    }
    place = {"gx": gx, "gy": gy}
    if n_x == 2:
        x_sides = [("gx", 1 - gx)]
    else:
        x_sides = [("gx", 0), ("gx", 1)]
    y_sides = [("gy", 0), ("gy", 1)]
    sides = [("gx", 0), ("gx", 1)] + y_sides
    peers = [lax.rem(gb + j, n_b) for j in range(1, n_b)]

    def target(side):
        axis, up = side
        return {axis: place[axis] + (2 * up - 1)}

    barrier = pltpu.get_barrier_semaphore()
    partners = n_b - 1
    for side in sides:
        partners = partners + has[side].astype(jnp.int32)

        @pl.when(has[side])
        def _():
            pl.semaphore_signal(barrier, inc=1, device_id=target(side), device_id_type=MESH)

    for peer in peers:
        pl.semaphore_signal(barrier, inc=1, device_id={"band": peer}, device_id_type=MESH)
    orb_in = pltpu.make_async_copy(orb_hbm, orb_ref, in_sem.at[0])
    orb_in.start()
    ext_in = pltpu.make_async_copy(ext_hbm, ext_ref, in_sem.at[1])
    ext_in.start()

    chunks = max(1, min(6, ny // 2))
    x_cuts = [(j * (ny // chunks), ny // chunks + (ny % chunks if j == chunks - 1 else 0)) for j in range(chunks)]
    mid = (nx - 4) // 2
    y_cuts = [(0, 2), (nx - 2, 2), (2, mid), (2 + mid, nx - 4 - mid)]
    d_cuts = [(0, 2), (ny - 2, 2), (2, ny - 4)]
    order = sorted(range(chunks), key=lambda j: 0 if j in (0, chunks - 1) else 1)
    sems = {"gx": (x_send, x_recv), "gy": (y_send, y_recv)}

    def cells(axis, edge, piece):
        if axis == "gx":
            return pl.ds(edge, 2), pl.ds(2 + x_cuts[piece][0], x_cuts[piece][1])
        return pl.ds(2 + y_cuts[piece][0], y_cuts[piece][1]), pl.ds(edge, 2)

    def pick(up, high, low):
        if isinstance(up, int):
            return high if up else low
        return low + up * (high - low)

    def send_copy(step, side, piece):
        axis, up = side
        extent = nx if axis == "gx" else ny
        return pltpu.make_async_remote_copy(
            src_ref=terms[step].at[cells(axis, pick(up, extent, 2), piece)],
            dst_ref=terms[step].at[cells(axis, pick(up, 0, extent + 2), piece)],
            send_sem=sems[axis][0].at[step, up, piece],
            recv_sem=sems[axis][1].at[step, 1 - up, piece],
            device_id=target(side),
            device_id_type=MESH,
        )

    def recv_copy(step, side, piece):
        axis, up = side
        extent = nx if axis == "gx" else ny
        land = terms[step].at[cells(axis, pick(up, extent + 2, 0), piece)]
        return pltpu.make_async_remote_copy(
            src_ref=land,
            dst_ref=land,
            send_sem=sems[axis][0].at[step, up, piece],
            recv_sem=sems[axis][1].at[step, up, piece],
            device_id=target(side),
            device_id_type=MESH,
        )

    def each(side, act):
        if side[0] == "gx" and n_x == 2:
            act()
        else:
            pl.when(has[side])(act)

    def start(step, side, pieces):
        def act():
            for piece in pieces:
                send_copy(step, side, piece).start()

        each(side, act)

    def await_pieces(step, side, pieces):
        def act():
            for piece in pieces:
                recv_copy(step, side, piece).wait_recv()

        each(side, act)

    def density_copy(which, j, piece):
        rows = pl.ds(*d_cuts[piece])
        return pltpu.make_async_remote_copy(
            src_ref=density.at[which, 0, rows],
            dst_ref=density.at[which, n_b - 1 - j, rows],
            send_sem=d_send.at[which, j, piece],
            recv_sem=d_recv.at[which, n_b - 2 - j, piece],
            device_id={"band": peers[j]},
            device_id_type=MESH,
        )

    def start_density(which, piece):
        for j in range(n_b - 1):
            density_copy(which, j, piece).start()

    def finish_potential(which):
        for piece in range(3):
            rows = pl.ds(*d_cuts[piece])
            for slot in range(1, n_b):
                pltpu.make_async_remote_copy(
                    src_ref=density.at[which, slot, rows],
                    dst_ref=density.at[which, slot, rows],
                    send_sem=d_send.at[which, slot - 1, piece],
                    recv_sem=d_recv.at[which, slot - 1, piece],
                    device_id={"band": peers[slot - 1]},
                    device_id_type=MESH,
                ).wait_recv()
        total = density[which, 0]
        for slot in range(1, n_b):
            total = total + density[which, slot]
        pot = ext_ref[...] - exchange_coef * cube_root(total)
        if which == 1:
            pot_ref[...] = pot
        wide = pot - 1.5 * centre_weight
        for y in range(ny):
            for x in range(nx):
                pot_wide[x, y] = jnp.broadcast_to(wide[y, x : x + 1], (nf, nz))

    for side in sides:
        axis, up = side

        @pl.when(jnp.logical_not(has[side]))
        def _():
            for step in range(8):
                if axis == "gx":
                    shape = (2, ny, nf, nz)
                    terms[step][pl.ds(nx + 2 if up else 0, 2), pl.ds(2, ny)] = jnp.zeros(shape, jnp.float32)
                else:
                    shape = (nx, 2, nf, nz)
                    terms[step][pl.ds(2, nx), pl.ds(ny + 2 if up else 0, 2)] = jnp.zeros(shape, jnp.float32)

    orb_in.wait()
    for y in range(ny):
        block = orb_ref[:, y]
        terms[0][pl.ds(2, nx), y + 2] = jnp.swapaxes(block, 0, 1)
        density[0, 0, y] = jnp.sum(block * block, axis=0)
    pl.semaphore_wait(barrier, partners)
    for side in x_sides:
        start(0, side, order)
    for side in y_sides:
        start(0, side, range(4))
    for piece in range(3):
        start_density(0, piece)
    ext_in.wait()

    lane = lax.broadcasted_iota(jnp.int32, (nf, nz), 1)
    near = -0.5 * near_weight
    far = -0.5 * far_weight
    below1 = jnp.where(lane >= 1, near, 0.0)
    above1 = jnp.where(lane < nz - 1, near, 0.0)
    below2 = jnp.where(lane >= 2, far, 0.0)
    above2 = jnp.where(lane < nz - 2, far, 0.0)
    half = nf // 2
    field = lax.broadcasted_iota(jnp.int32, (nf, nz), 0)
    turn_sign = jnp.where(field < half, 1.0, -1.0)

    def turned(v):
        return jnp.concatenate([v[half:], v[:half]], axis=0) * turn_sign

    def image(step, x, y):
        t = terms[step]
        c = t[x + 2, y + 2]
        one = (t[x + 1, y + 2] + t[x + 3, y + 2]) + (
            t[x + 2, y + 1] + t[x + 2, y + 3]
        )
        two = (t[x, y + 2] + t[x + 4, y + 2]) + (
            t[x + 2, y] + t[x + 2, y + 4]
        )
        total = pot_wide[x, y] * c + near * one + far * two
        total = total + pltpu.roll(c, 1, 1) * below1 + pltpu.roll(c, nz - 1, 1) * above1
        return total + (pltpu.roll(c, 2, 1) * below2 + pltpu.roll(c, nz - 2, 1) * above2)

    def combine(parts, s):
        even = parts[0] + (-(s**2) / 2) * parts[2] + (s**4 / 24) * parts[4]
        odd = s * parts[1] + (-(s**3) / 6) * parts[3]
        return even + turned(odd)

    def advance(step, xs, ys):
        at = [(x, y) for x in xs for y in ys]
        new = [image(step, x, y) for x, y in at]
        if step % 4 < 3:
            for (x, y), value in zip(at, new):
                terms[step + 1][x + 2, y + 2] = value
            return
        parts = [[terms[step - 3 + k][x + 2, y + 2] for k in range(4)] + [value] for (x, y), value in zip(at, new)]
        halves = [combine(part, step_length / 2) for part in parts]
        if step == 7:
            for (x, y), value in zip(at, halves):
                out_ref[x, y] = value
            return
        predicted = [combine(part, step_length) for part in parts]
        squares = [jnp.sum(value * value, axis=0, keepdims=True) for value in predicted]
        for (x, y), value, square in zip(at, halves, squares):
            terms[4][x + 2, y + 2] = value
            density[1, 0, y, pl.ds(x, 1)] = square

    rim = [0, 1, nx - 2, nx - 1]
    for step in range(8):
        if step % 4 == 0:
            finish_potential(step // 4)
        for n, j in enumerate(order):
            edges = [("gy", up) for up, at in ((0, 0), (1, chunks - 1)) if at == j]
            for side in x_sides:
                await_pieces(step, side, [j])
            for side in edges:
                await_pieces(step, side, [0, 1])
            advance(step, rim, range(x_cuts[j][0], sum(x_cuts[j])))
            if step < 7:
                for side in x_sides:
                    start(step + 1, side, [j])
                for side in edges:
                    start(step + 1, side, [0, 1])
            if n == min(1, chunks - 1):
                for piece in (2, 3):
                    for side in y_sides:
                        await_pieces(step, side, [piece])
                    advance(step, range(y_cuts[piece][0], sum(y_cuts[piece])), [0, 1, ny - 2, ny - 1])
                    if step < 7:
                        for side in y_sides:
                            start(step + 1, side, [piece])
                if step == 3:
                    start_density(1, 0)
                    start_density(1, 1)
        for x in range(2, nx - 2):
            advance(step, [x], range(2, ny - 2))
        if step == 3:
            start_density(1, 2)

    for side in x_sides + y_sides:

        def drain():
            for step in range(8):
                for piece in range(chunks if side[0] == "gx" else 4):
                    send_copy(step, side, piece).wait_send()

        each(side, drain)

    for which in (0, 1):
        for j in range(n_b - 1):
            for piece in range(3):
                density_copy(which, j, piece).wait_send()


def body(counts, orbitals, external):
    parts, bands, nx, ny, nz = orbitals.shape
    nf = parts * bands
    fields = jnp.transpose(orbitals.reshape(nf, nx, ny, nz), (0, 2, 1, 3))
    n_b = counts[2]
    dma = pltpu.SemaphoreType.DMA
    result, potential = pl.pallas_call(
        functools.partial(kernel, counts),
        out_shape=(
            jax.ShapeDtypeStruct((nx, ny, nf, nz), jnp.float32),
            jax.ShapeDtypeStruct((ny, nx, nz), jnp.float32),
        ),
        in_specs=[pl.BlockSpec(memory_space=pltpu.HBM)] * 2,
        out_specs=(pl.BlockSpec(memory_space=pltpu.VMEM),) * 2,
        scratch_shapes=[
            *[pltpu.VMEM((nx + 4, ny + 4, nf, nz), jnp.float32)] * 8,
            pltpu.VMEM((nf, ny, nx, nz), jnp.float32),
            pltpu.VMEM((ny, nx, nz), jnp.float32),
            pltpu.VMEM((nx, ny, nf, nz), jnp.float32),
            pltpu.VMEM((2, n_b, ny, nx, nz), jnp.float32),
            dma((2,)),
            dma((8, 2, 6)),
            dma((8, 2, 6)),
            dma((8, 2, 4)),
            dma((8, 2, 4)),
            dma((2, n_b - 1, 3)),
            dma((2, n_b - 1, 3)),
        ],
        compiler_params=pltpu.CompilerParams(
            collective_id=0, has_side_effects=True, vmem_limit_bytes=40 * 1024 * 1024
        ),
    )(fields, jnp.swapaxes(external, 0, 1))
    result = jnp.transpose(result, (2, 0, 1, 3)).reshape(orbitals.shape)
    return (result, jnp.swapaxes(potential, 0, 1))


def solution(mesh):
    counts = (mesh.shape["gx"], mesh.shape["gy"], mesh.shape["band"])
    in_specs = (P(None, "band", "gx", "gy", None), P("gx", "gy", None))
    out_specs = (P(None, "band", "gx", "gy", None), P("gx", "gy", None))
    return jax.shard_map(
        functools.partial(body, counts), mesh=mesh, in_specs=in_specs, out_specs=out_specs, check_vma=False
    )
```

profile of v0, /device:TPU:0, one launch (start us, length us, event | category | flops | bytes accessed | tf_op | source)
XLA Modules:
  0.0 40.5 jit_solution(6024102643655280447)
XLA Ops:
  0.6 0.0 copy-start
  0.6 1.0 %copy-done = f32[2,4,8,12,128]{4,2,3,1,0:T(8,128)S(1)} copy-done((f32[2,4,8,12,128]{4,2,3,1,0:T(8,128)S(1)}, f32[2,4,8,12,128]{4,2,3,1,0:T(8,128)}, u32[]{:S(2)}) %copy-start) | copy-done | bytes 393240
  1.6 0.0 copy-start.1
  1.6 0.8 %copy-done.1 = f32[8,12,128]{2,0,1:T(8,128)S(1)} copy-done((f32[8,12,128]{2,0,1:T(8,128)S(1)}, f32[8,12,128]{2,0,1:T(8,128)}, u32[]{:S(2)}) %copy-start.1) | copy-done | bytes 49176
  2.4 36.5 %shard_map.41 = (f32[8,12,8,128]{3,2,1,0:T(8,128)S(1)}, f32[12,8,128]{2,1,0:T(8,128)S(1)}) custom-call(f32[8,12,8,128]{3,2,1,0:T(8,128)S(1)} %bitcast.8, f32[12,8,128]{2,1,0:T(8,128)S(1)} %bitcast.10), custom_call_target="tpu_custom_call" | custom-call | tf_op jit(solution)/shard_map/pallas_call | solution.py:299
  38.9 1.0 %copy.4 = f32[2,4,8,12,128]{4,2,3,1,0:T(8,128)} copy(f32[2,4,8,12,128]{4,1,0,3,2:T(4,128)S(1)} %bitcast.9) | data formatting | bytes 786432
  39.9 0.6 %copy.6 = f32[8,12,128]{2,0,1:T(8,128)} copy(f32[8,12,128]{2,0,1:T(8,128)S(1)} %bitcast.11) | data formatting | bytes 98304
Async XLA Ops:
  0.6 1.0 %copy-start = (f32[2,4,8,12,128]{4,2,3,1,0:T(8,128)S(1)}, f32[2,4,8,12,128]{4,2,3,1,0:T(8,128)}, u32[]{:S(2)}) copy-start(f32[2,4,8,12,128]{4,2,3,1,0:T(8,128)} %param.2) | copy-start | bytes 1179652
  1.6 0.8 %copy-start.1 = (f32[8,12,128]{2,0,1:T(8,128)S(1)}, f32[8,12,128]{2,0,1:T(8,128)}, u32[]{:S(2)}) copy-start(f32[8,12,128]{2,0,1:T(8,128)} %param.3) | copy-start | bytes 147460
where the time goes:
time: 40.7 us; the launch traced here: 40.5 us
  Pallas kernels  36.5 us (90%)
  local copies, waits for them, and re-layouts  3.38 us (8%)
  between operations  0.65 us (2%)
    pallas_call x1, Pallas kernels, body(): pl.pallas_call(functools.partial(kernel, counts), out_shape=(jax.ShapeDty...  36.5 us
    unnamed x6, local copies, waits for them, and re-layouts  3.38 us

commit v1 on v0

--- a/solution.py
+++ b/solution.py
@@ -21,7 +21,7 @@
     return jnp.where(d > 1e-30, better, guess)
 
 
-def kernel(counts, orb_hbm, ext_hbm, out_ref, pot_ref, *scratch):
+def step_kernel(counts, orb_hbm, ext_hbm, out_ref, pot_ref, *scratch):
     terms = scratch[:8]
     orb_ref, ext_ref, pot_wide, density, in_sem, x_send, x_recv, y_send, y_recv, d_send, d_recv = scratch[8:]
     n_x, n_y, n_b = counts
@@ -290,14 +290,14 @@
                 density_copy(which, j, piece).wait_send()
 
 
-def body(counts, orbitals, external):
+def step_body(counts, orbitals, external):
     parts, bands, nx, ny, nz = orbitals.shape
     nf = parts * bands
     fields = jnp.transpose(orbitals.reshape(nf, nx, ny, nz), (0, 2, 1, 3))
     n_b = counts[2]
     dma = pltpu.SemaphoreType.DMA
     result, potential = pl.pallas_call(
-        functools.partial(kernel, counts),
+        functools.partial(step_kernel, counts),
         out_shape=(
             jax.ShapeDtypeStruct((nx, ny, nf, nz), jnp.float32),
             jax.ShapeDtypeStruct((ny, nx, nz), jnp.float32),
@@ -326,6 +326,517 @@
     return (result, jnp.swapaxes(potential, 0, 1))
 
 
+DEEP = 8
+VDEEP = 6
+
+
+def whole_kernel(counts, orb_hbm, ext_hbm, out_ref, pot_ref, *scratch):
+    (
+        psi, half, t1, t2, t3, orb_v, ext_all, v_now, v_next, dens, chip_in, chip_sum, plane_in, partial, swap_in,
+        pieces_in, done, result, in_sem, x_send, x_recv, z_send, z_recv, f_send, f_recv, h_send, h_recv,
+        a_send, a_recv, b_send, b_recv, c_send, c_recv, e_send, e_recv, r_send, r_recv, l_sem,
+    ) = scratch
+    n_x, n_y, n_b = counts
+    parts, nb, ny, nx, nz = orb_hbm.shape
+    own = nb // 2
+    mid = ny // 2
+    gx = lax.axis_index("gx")
+    gy = lax.axis_index("gy")
+    gb = lax.axis_index("band")
+    ox = 1 - gx
+    core = lax.rem(gb, 2)
+    mate = gb + 1 - 2 * core
+    far_gb = lax.rem(gb + 2, n_b)
+    has = (gy > 0, gy < n_y - 1)
+    edge = 8
+    here = pl.ds(pl.multiple_of(nx * gx, nx), nx)
+    there = pl.ds(pl.multiple_of(nx * ox, nx), nx)
+    here_pad = pl.ds(pl.multiple_of(edge + nx * gx, 8), nx)
+    there_pad = pl.ds(pl.multiple_of(edge + nx * ox, 8), nx)
+
+    def z_peer(d):
+        return gy + (2 * d - 1)
+
+    in_plane = [{"band": mate}, {"band": far_gb}, {"gx": ox}, {"gx": ox, "band": mate}, {"gx": ox, "band": far_gb}]
+    barrier = pltpu.get_barrier_semaphore()
+    partners = len(in_plane)
+    for peer in in_plane:
+        pl.semaphore_signal(barrier, inc=1, device_id=peer, device_id_type=MESH)
+    for d in (0, 1):
+        partners = partners + 4 * has[d].astype(jnp.int32)
+
+        @pl.when(has[d])
+        def _():
+            for x in (gx, ox):
+                for b in (gb, mate):
+                    pl.semaphore_signal(
+                        barrier, inc=1, device_id={"gx": x, "gy": z_peer(d), "band": b}, device_id_type=MESH
+                    )
+
+    give = pl.ds(pl.multiple_of(own * ox, own), own)
+    keep = pl.ds(pl.multiple_of(own * gx, own), own)
+    give_in = pltpu.make_async_copy(orb_hbm.at[:, give], orb_v.at[:, give], in_sem.at[0])
+    keep_in = pltpu.make_async_copy(orb_hbm.at[:, keep], orb_v.at[:, keep], in_sem.at[1])
+    ext_in = pltpu.make_async_copy(ext_hbm, ext_all.at[:, here], in_sem.at[2])
+    psi_in = pltpu.make_async_copy(
+        orb_hbm.at[:, keep], psi.at[:, :, pl.ds(DEEP, ny), here_pad], in_sem.at[3]
+    )
+    give_in.start()
+    keep_in.start()
+    ext_in.start()
+    psi_in.start()
+
+    def remote(src, dst, send, recv, peer):
+        return pltpu.make_async_remote_copy(
+            src_ref=src, dst_ref=dst, send_sem=send, recv_sem=recv, device_id=peer, device_id_type=MESH
+        )
+
+    quarter = 4
+    pieces = list(range(ny // quarter))
+    goes = ([q for q in pieces if quarter * q < DEEP], [q for q in pieces if quarter * q >= ny - DEEP])
+    piece_order = sorted(pieces, key=lambda q: 0 if q in goes[0] and q in goes[1] else 1)
+
+    def x_copy(j, q):
+        return remote(
+            orb_v.at[:, own * ox + j, pl.ds(quarter * q, quarter)],
+            psi.at[:, j, pl.ds(DEEP + quarter * q, quarter), here_pad],
+            x_send.at[j, q], x_recv.at[j, q], {"gx": ox},
+        )
+
+    def x_land(j, q):
+        land = psi.at[:, j, pl.ds(DEEP + quarter * q, quarter), there_pad]
+        return remote(land, land, x_send.at[j, q], x_recv.at[j, q], {"gx": ox})
+
+    def halo_row(d):
+        return 0 if d else DEEP + ny
+
+    def z_copy(j, d):
+        return remote(
+            orb_v.at[:, own * gx + j, pl.ds(ny - DEEP if d else 0, DEEP)],
+            psi.at[:, j, pl.ds(halo_row(d), DEEP), here_pad],
+            z_send.at[d, j], z_recv.at[d, j], {"gy": z_peer(d)},
+        )
+
+    def z_land(j, d):
+        land = psi.at[:, j, pl.ds(halo_row(d), DEEP), here_pad]
+        return remote(land, land, z_send.at[d, j], z_recv.at[d, j], {"gy": z_peer(1 - d)})
+
+    def f_row(d, q):
+        return DEEP + quarter * q + (-ny if d else ny)
+
+    def f_copy(j, d, q):
+        return remote(
+            psi.at[:, j, pl.ds(DEEP + quarter * q, quarter), there_pad],
+            psi.at[:, j, pl.ds(f_row(d, q), quarter), there_pad],
+            f_send.at[d, j, q], f_recv.at[d, j, q], {"gy": z_peer(d)},
+        )
+
+    def f_land(j, d, q):
+        land = psi.at[:, j, pl.ds(f_row(d, q), quarter), there_pad]
+        return remote(land, land, f_send.at[d, j, q], f_recv.at[d, j, q], {"gy": z_peer(1 - d)})
+
+    def h_copy(j, d):
+        return remote(
+            half.at[:, j, pl.ds(ny if d else DEEP, DEEP), pl.ds(edge, 2 * nx)],
+            half.at[:, j, pl.ds(halo_row(d), DEEP), pl.ds(edge, 2 * nx)],
+            h_send.at[d, j], h_recv.at[d, j], {"gy": z_peer(d)},
+        )
+
+    def h_land(j, d):
+        land = half.at[:, j, pl.ds(halo_row(d), DEEP), pl.ds(edge, 2 * nx)]
+        return remote(land, land, h_send.at[d, j], h_recv.at[d, j], {"gy": z_peer(1 - d)})
+
+    zero = jnp.zeros((8, nz), jnp.float32)
+    rows_all = ny + 2 * DEEP
+
+    def clear(r, _):
+        for p in range(parts):
+            for j in range(own):
+                for ref in (psi, half, t1, t2, t3):
+                    ref[p, j, r, pl.ds(0, 8)] = zero
+                    ref[p, j, r, pl.ds(edge + 2 * nx, 8)] = zero
+        return 0
+
+    lax.fori_loop(0, rows_all, clear, 0)
+    for d in (0, 1):
+
+        @pl.when(jnp.logical_not(has[d]))
+        def _():
+            def clear_row(i, _):
+                r = i + halo_row(1 - d)
+                for p in range(parts):
+                    for j in range(own):
+                        for ref in (psi, half, t1, t2, t3):
+                            for x in range(0, 2 * nx, 8):
+                                ref[p, j, r, pl.ds(edge + x, 8)] = zero
+                return 0
+
+            lax.fori_loop(0, DEEP, clear_row, 0)
+
+    give_in.wait()
+    keep_in.wait()
+    pl.semaphore_wait(barrier, partners)
+    for j in range(own):
+        for q in piece_order:
+            x_copy(j, q).start()
+    for d in (0, 1):
+
+        @pl.when(has[d])
+        def _():
+            for j in range(own):
+                z_copy(j, d).start()
+
+    for y in range(ny):
+        total = None
+        for p in range(parts):
+            for j in range(nb):
+                v = orb_v[p, j, y]
+                total = v * v if total is None else total + v * v
+        dens[y] = total
+    first = remote(dens, chip_in, a_send.at[0], a_recv.at[0], {"band": mate})
+    first.start()
+    ext_in.wait()
+    first.wait_recv()
+    my_rows = pl.ds(mid * core, mid)
+    chip_sum[...] = dens[my_rows] + chip_in[my_rows]
+    second = remote(chip_sum, plane_in, b_send.at[0], b_recv.at[0], {"band": far_gb})
+    second.start()
+
+    def forward(j, q):
+        x_land(j, q).wait_recv()
+        for d in (0, 1):
+            if q in goes[d]:
+
+                @pl.when(has[d])
+                def _():
+                    f_copy(j, d, q).start()
+
+    todo = [(j, q) for j in range(own) for q in piece_order]
+    forward(*todo[0])
+    second.wait_recv()
+    shift = -1.5 * centre_weight
+    v_rows = pl.ds(VDEEP + mid * core, mid)
+    v_now[v_rows, here] = ext_all[my_rows, here] - exchange_coef * cube_root(chip_sum[...] + plane_in[...]) + shift
+
+    own_slot = v_now.at[v_rows, here]
+    to_mate = remote(own_slot, own_slot, c_send.at[0, 0], c_recv.at[0, 0], {"band": mate})
+    to_x = [
+        remote(own_slot, own_slot, c_send.at[0, 1 + n], c_recv.at[0, 1 + core], {"gx": ox, "band": b})
+        for n, b in enumerate((gb, mate))
+    ]
+    z_src = v_now.at[pl.ds(VDEEP + core * (ny - VDEEP), VDEEP), here]
+    z_dst = v_now.at[pl.ds((1 - core) * (ny + VDEEP), VDEEP), here]
+    z_to = gy + 2 * core - 1
+    z_ok = jnp.logical_and(z_to >= 0, z_to < n_y)
+    to_z = [
+        remote(
+            z_src, z_dst, c_send.at[0, 3 + 2 * m + n], c_recv.at[0, 5 - 2 * core + m],
+            {"gx": x, "gy": z_to, "band": b},
+        )
+        for m, x in enumerate((gx, ox))
+        for n, b in enumerate((gb, mate))
+    ]
+    for copy in to_x:
+        copy.start()
+
+    @pl.when(z_ok)
+    def _():
+        for copy in to_z[2:] + to_z[:2]:
+            copy.start()
+
+    to_mate.start()
+    ext_here, ext_there = ext_all.at[:, here], ext_all.at[:, there]
+    ext_over = remote(ext_here, ext_here, e_send.at[0], e_recv.at[0], {"gx": ox})
+    ext_over.start()
+    for pair in todo[1:]:
+        forward(*pair)
+
+    def v_wait(ref, which, slot, rows, cols):
+        land = ref.at[rows, cols]
+        remote(land, land, c_send.at[which, slot], c_recv.at[which, slot], {"band": mate}).wait_recv()
+
+    v_wait(v_now, 0, 0, pl.ds(VDEEP + mid * (1 - core), mid), here)
+    for c in (0, 1):
+        v_wait(v_now, 0, 1 + c, pl.ds(VDEEP + mid * c, mid), there)
+    for side in (0, 1):
+
+        @pl.when(has[side])
+        def _():
+            rows = pl.ds(side * (ny + VDEEP), VDEEP)
+            v_wait(v_now, 0, 3 + 2 * side, rows, here)
+            v_wait(v_now, 0, 4 + 2 * side, rows, there)
+
+    psi_in.wait()
+
+    lane = lax.broadcasted_iota(jnp.int32, (8, nz), 1)
+    near = -0.5 * near_weight
+    far = -0.5 * far_weight
+    below1 = jnp.where(lane >= 1, near, 0.0)
+    above1 = jnp.where(lane < nz - 1, near, 0.0)
+    below2 = jnp.where(lane >= 2, far, 0.0)
+    above2 = jnp.where(lane < nz - 2, far, 0.0)
+
+    def image(src, v, p, j, r, x):
+        def at(row, col):
+            return src[p, j, row, pl.ds(edge + col, 8)]
+
+        c = at(r, x)
+        one = (at(r, x - 1) + at(r, x + 1)) + (at(r - 1, x) + at(r + 1, x))
+        two = (at(r, x - 2) + at(r, x + 2)) + (at(r - 2, x) + at(r + 2, x))
+        total = v * c + near * one + far * two
+        total = total + pltpu.roll(c, 1, 1) * below1 + pltpu.roll(c, nz - 1, 1) * above1
+        return total + (pltpu.roll(c, 2, 1) * below2 + pltpu.roll(c, nz - 2, 1) * above2)
+
+    cols = range(0, 2 * nx, 8)
+
+    def level(src, dst, pot, j, first_row, count):
+        for i in range(count):
+            r = first_row + i
+            for x in cols:
+                v = pot[r - DEEP + VDEEP, pl.ds(x, 8)]
+                for p in range(parts):
+                    dst[p, j, r, pl.ds(edge + x, 8)] = image(src, v, p, j, r, x)
+
+    def rows_of(src, dst, pot, j, first_row, count, group):
+        def some(i, _):
+            level(src, dst, pot, j, first_row + i * group, group)
+            return 0
+
+        lax.fori_loop(0, count // group, some, 0)
+
+    def chain(start, pot, j):
+        for src, dst, deep in ((start, t1, 6), (t1, t2, 4), (t2, t3, 2)):
+            for side in (0, 1):
+
+                @pl.when(has[side])
+                def _():
+                    rows_of(src, dst, pot, j, DEEP + ny if side else DEEP - deep, deep, 2)
+
+            rows_of(src, dst, pot, j, DEEP, ny, 4)
+
+    def last(start, pot, j, r, x, act):
+        v = pot[r - DEEP + VDEEP, pl.ds(x, 8)]
+        ts = [[t[p, j, r, pl.ds(edge + x, 8)] for t in (start, t1, t2, t3)] for p in range(parts)]
+        for p in range(parts):
+            ts[p].append(image(t3, v, p, j, r, x))
+
+        def combine(s):
+            even = [ts[p][0] + (-(s**2) / 2) * ts[p][2] + (s**4 / 24) * ts[p][4] for p in range(2)]
+            odd = [s * ts[p][1] + (-(s**3) / 6) * ts[p][3] for p in range(2)]
+            return even[0] + odd[1], even[1] - odd[0]
+
+        act(combine)
+
+    for j in range(own):
+        for side in (0, 1):
+
+            @pl.when(has[side])
+            def _():
+                d = 1 - side
+                z_land(j, d).wait_recv()
+                for q in goes[d]:
+                    f_land(j, d, q).wait_recv()
+
+        chain(psi, v_now, j)
+
+        def finish_row(i, _):
+            for k in range(2):
+                y = 2 * i + k
+                r = DEEP + y
+                for x in cols:
+
+                    def act(combine):
+                        for p, value in enumerate(combine(step_length / 2)):
+                            half[p, j, r, pl.ds(edge + x, 8)] = value
+                        a, b = combine(step_length)
+                        square = a * a + b * b
+                        if j:
+                            square = square + partial[y, pl.ds(x, 8)]
+                        partial[y, pl.ds(x, 8)] = square
+
+                    last(psi, v_now, j, r, x, act)
+            return 0
+
+        lax.fori_loop(0, ny // 2, finish_row, 0)
+        if j == own - 1:
+            mine = pl.ds(pl.multiple_of(nx * core, nx), nx)
+            theirs = pl.ds(pl.multiple_of(nx * (1 - core), nx), nx)
+            third = remote(partial.at[:, theirs], swap_in, a_send.at[1], a_recv.at[1], {"band": mate})
+            third.start()
+        for d in (0, 1):
+
+            @pl.when(has[d])
+            def _():
+                h_copy(j, d).start()
+
+    third.wait_recv()
+    done[...] = partial[:, mine] + swap_in[...]
+    spread = [
+        remote(done, pieces_in.at[n], b_send.at[1 + n], b_recv.at[1 + n], peer)
+        for n, peer in enumerate(({"gx": ox}, {"band": far_gb}, {"gx": ox, "band": far_gb}))
+    ]
+    for copy in (spread[2], spread[0], spread[1]):
+        copy.start()
+    remote(ext_there, ext_there, e_send.at[0], e_recv.at[0], {"gx": ox}).wait_recv()
+    for copy in spread:
+        copy.wait_recv()
+    total = (done[...] + pieces_in[0]) + (pieces_in[1] + pieces_in[2])
+    v_next[pl.ds(VDEEP, ny), mine] = ext_all[:, mine] - exchange_coef * cube_root(total) + shift
+    next_z = []
+    for d in (0, 1):
+        z_src = v_next.at[pl.ds(ny if d else VDEEP, VDEEP), mine]
+        z_dst = v_next.at[pl.ds(0 if d else ny + VDEEP, VDEEP), mine]
+        copies = [
+            remote(z_src, z_dst, c_send.at[1, 1 + 2 * d + n], c_recv.at[1, 1 + 2 * d + core], {"gy": z_peer(d), "band": b})
+            for n, b in enumerate((gb, mate))
+        ]
+        next_z.append(copies)
+
+        @pl.when(has[d])
+        def _():
+            for copy in copies:
+                copy.start()
+
+    whole = v_next.at[pl.ds(VDEEP, ny), mine]
+    next_mate = remote(whole, whole, c_send.at[1, 0], c_recv.at[1, 0], {"band": mate})
+    next_mate.start()
+    v_wait(v_next, 1, 0, pl.ds(VDEEP, ny), theirs)
+    pot_ref[...] = v_next[pl.ds(VDEEP, ny), here] - shift
+    for side in (0, 1):
+
+        @pl.when(has[side])
+        def _():
+            d = 1 - side
+            rows = pl.ds(side * (ny + VDEEP), VDEEP)
+            for c in (0, 1):
+                v_wait(v_next, 1, 1 + 2 * d + c, rows, pl.ds(nx * c, nx))
+
+    def back_copy(j, q):
+        rows = pl.ds(quarter * q, quarter)
+        return remote(
+            result.at[:, j, rows, there],
+            out_ref.at[:, own * gx + j, rows],
+            r_send.at[j, q], r_recv.at[j, q], {"gx": ox},
+        )
+
+    def back_land(j, q):
+        land = out_ref.at[:, own * ox + j, pl.ds(quarter * q, quarter)]
+        return remote(land, land, r_send.at[j, q], r_recv.at[j, q], {"gx": ox})
+
+    def stay_copy(j, q):
+        rows = pl.ds(quarter * q, quarter)
+        return pltpu.make_async_copy(result.at[:, j, rows, here], out_ref.at[:, own * gx + j, rows], l_sem.at[j, q])
+
+    for j in range(own):
+        for side in (0, 1):
+
+            @pl.when(has[side])
+            def _():
+                h_land(j, 1 - side).wait_recv()
+
+        chain(half, v_next, j)
+        for q in pieces:
+            for k in range(quarter):
+                y = quarter * q + k
+                for x in cols:
+
+                    def act(combine):
+                        for p, value in enumerate(combine(step_length / 2)):
+                            result[p, j, y, pl.ds(x, 8)] = value
+
+                    last(half, v_next, j, DEEP + y, x, act)
+            back_copy(j, q).start()
+            stay_copy(j, q).start()
+
+    first.wait_send()
+    second.wait_send()
+    third.wait_send()
+    to_mate.wait_send()
+    ext_over.wait_send()
+    next_mate.wait_send()
+    for copy in to_x + spread:
+        copy.wait_send()
+
+    @pl.when(z_ok)
+    def _():
+        for copy in to_z:
+            copy.wait_send()
+
+    for d in (0, 1):
+
+        @pl.when(has[d])
+        def _():
+            for copy in next_z[d]:
+                copy.wait_send()
+            for j in range(own):
+                z_copy(j, d).wait_send()
+                h_copy(j, d).wait_send()
+                for q in goes[d]:
+                    f_copy(j, d, q).wait_send()
+
+    for j in range(own):
+        for q in pieces:
+            x_copy(j, q).wait_send()
+            back_copy(j, q).wait_send()
+            stay_copy(j, q).wait()
+            back_land(j, q).wait_recv()
+
+
+def whole_body(counts, orbitals, external):
+    parts, nb, nx, ny, nz = orbitals.shape
+    own = nb // 2
+    nq = ny // 4
+    dma = pltpu.SemaphoreType.DMA
+    term = pltpu.VMEM((parts, own, ny + 2 * DEEP, 2 * nx + 16, nz), jnp.float32)
+    block = pltpu.VMEM((ny, nx, nz), jnp.float32)
+    half_block = pltpu.VMEM((ny // 2, nx, nz), jnp.float32)
+    wide = pltpu.VMEM((ny + 2 * VDEEP, 2 * nx, nz), jnp.float32)
+    result, potential = pl.pallas_call(
+        functools.partial(whole_kernel, counts),
+        out_shape=(
+            jax.ShapeDtypeStruct((parts, nb, ny, nx, nz), jnp.float32),
+            jax.ShapeDtypeStruct((ny, nx, nz), jnp.float32),
+        ),
+        in_specs=[pl.BlockSpec(memory_space=pltpu.HBM)] * 2,
+        out_specs=(pl.BlockSpec(memory_space=pltpu.VMEM),) * 2,
+        scratch_shapes=[
+            term, term, term, term, term,
+            pltpu.VMEM((parts, nb, ny, nx, nz), jnp.float32),
+            pltpu.VMEM((ny, 2 * nx, nz), jnp.float32),
+            wide, wide,
+            block, block, half_block, half_block,
+            pltpu.VMEM((ny, 2 * nx, nz), jnp.float32),
+            block,
+            pltpu.VMEM((3, ny, nx, nz), jnp.float32),
+            block,
+            pltpu.VMEM((parts, own, ny, 2 * nx, nz), jnp.float32),
+            dma((4,)),
+            dma((own, nq)), dma((own, nq)),
+            dma((2, own)), dma((2, own)),
+            dma((2, own, nq)), dma((2, own, nq)),
+            dma((2, own)), dma((2, own)),
+            dma((2,)), dma((2,)),
+            dma((4,)), dma((4,)),
+            dma((2, 7)), dma((2, 7)),
+            dma((1,)), dma((1,)),
+            dma((own, nq)), dma((own, nq)),
+            dma((own, nq)),
+        ],
+        compiler_params=pltpu.CompilerParams(
+            collective_id=0, has_side_effects=True, vmem_limit_bytes=60 * 1024 * 1024
+        ),
+    )(jnp.transpose(orbitals, (0, 1, 3, 2, 4)), jnp.swapaxes(external, 0, 1))
+    return jnp.transpose(result, (0, 1, 3, 2, 4)), jnp.swapaxes(potential, 0, 1)
+
+
+def body(counts, orbitals, external):
+    parts, nb, nx, ny, nz = orbitals.shape
+    n_x, n_y, n_b = counts
+    if n_x == 2 and n_b == 4 and nb % 2 == 0 and nx % 8 == 0 and ny % 4 == 0 and ny >= 2 * VDEEP:
+        return whole_body(counts, orbitals, external)
+    return step_body(counts, orbitals, external)
+
+
 def solution(mesh):
     counts = (mesh.shape["gx"], mesh.shape["gy"], mesh.shape["band"])
     in_specs = (P(None, "band", "gx", "gy", None), P("gx", "gy", None))

time: 40.7 us -> 41.7 us (1.025)
  Pallas kernels: 36.5 us -> 38.5 us
  local copies, waits for them, and re-layouts: 3.38 us -> 2.41 us
    pallas_call x1, Pallas kernels: 36.5 us -> 38.5 us  [whole_body(): pl.pallas_call(functools.partial(whole_kernel, counts), out_shape=(jax.Sh...]
    unnamed x6 -> x4, local copies, waits for them, and re-layouts: 3.38 us -> 2.41 us
where the time goes in v1:
time: 41.7 us; the launch traced here: 41.6 us
  Pallas kernels  38.5 us (92%)
  local copies, waits for them, and re-layouts  2.41 us (6%)
  between operations  0.65 us (2%)
    pallas_call x1, Pallas kernels, whole_body(): pl.pallas_call(functools.partial(whole_kernel, counts), out_shape=(jax.Sh...  38.5 us
    unnamed x4, local copies, waits for them, and re-layouts  2.41 us

profile of v1, /device:TPU:0, one launch (start us, length us, event | category | flops | bytes accessed | tf_op | source)
XLA Modules:
  0.0 41.6 jit_solution(4372948936442522716)
XLA Ops:
  0.6 38.5 %shard_map.41 = (f32[2,4,12,8,128]{4,3,2,1,0:T(8,128)}, f32[12,8,128]{2,1,0:T(8,128)}) custom-call(f32[2,4,12,8,128]{4,3,2,1,0:T(8,128)} %bitcast.4, f32[12,8,128]{2,1,0:T(8,128)} %bitcast.6), custom_call_target="tpu_custom_call" | custom-call | tf_op jit(solution)/shard_map/pallas_call | solution.py:794
  39.1 0.0 copy-start
  39.2 1.8 %copy.6 = f32[2,4,8,12,128]{4,2,3,1,0:T(8,128)} copy(f32[2,4,8,12,128]{4,2,3,1,0:T(8,128)} %bitcast.5) | data formatting | bytes 786432
  40.9 0.0 copy-done
  40.9 0.6 %copy.7 = f32[8,12,128]{2,0,1:T(8,128)} copy(f32[8,12,128]{2,0,1:T(8,128)S(1)} %bitcast.7) | data formatting | bytes 98304
Async XLA Ops:
  39.1 1.8 %copy-start = (f32[12,8,128]{2,1,0:T(8,128)S(1)}, f32[12,8,128]{2,1,0:T(8,128)}, u32[]{:S(2)}) copy-start(f32[12,8,128]{2,1,0:T(8,128)} %get-tuple-element.5) | copy-start | bytes 147460

commit v2 on v1

--- a/solution.py
+++ b/solution.py
@@ -328,13 +328,14 @@
 
 DEEP = 8
 VDEEP = 6
+SCALE = 24.0
 
 
 def whole_kernel(counts, orb_hbm, ext_hbm, out_ref, pot_ref, *scratch):
     (
         psi, half, t1, t2, t3, orb_v, ext_all, v_now, v_next, dens, chip_in, chip_sum, plane_in, partial, swap_in,
-        pieces_in, done, result, in_sem, x_send, x_recv, z_send, z_recv, f_send, f_recv, h_send, h_recv,
-        a_send, a_recv, b_send, b_recv, c_send, c_recv, e_send, e_recv, r_send, r_recv, l_sem,
+        pieces_in, done, result, weights, in_sem, x_send, x_recv, z_send, z_recv, f_send, f_recv, h_send, h_recv,
+        a_send, a_recv, b_send, b_recv, c_send, c_recv, e_send, e_recv, r_send, r_recv, l_sem, ready,
     ) = scratch
     n_x, n_y, n_b = counts
     parts, nb, ny, nx, nz = orb_hbm.shape
@@ -357,21 +358,17 @@
     def z_peer(d):
         return gy + (2 * d - 1)
 
-    in_plane = [{"band": mate}, {"band": far_gb}, {"gx": ox}, {"gx": ox, "band": mate}, {"gx": ox, "band": far_gb}]
+    in_plane = [{"band": mate}, {"band": far_gb}, {"gx": ox}]
     barrier = pltpu.get_barrier_semaphore()
     partners = len(in_plane)
     for peer in in_plane:
         pl.semaphore_signal(barrier, inc=1, device_id=peer, device_id_type=MESH)
     for d in (0, 1):
-        partners = partners + 4 * has[d].astype(jnp.int32)
+        partners = partners + has[d].astype(jnp.int32)
 
         @pl.when(has[d])
         def _():
-            for x in (gx, ox):
-                for b in (gb, mate):
-                    pl.semaphore_signal(
-                        barrier, inc=1, device_id={"gx": x, "gy": z_peer(d), "band": b}, device_id_type=MESH
-                    )
+            pl.semaphore_signal(barrier, inc=1, device_id={"gy": z_peer(d)}, device_id_type=MESH)
 
     give = pl.ds(pl.multiple_of(own * ox, own), own)
     keep = pl.ds(pl.multiple_of(own * gx, own), own)
@@ -446,6 +443,9 @@
         land = half.at[:, j, pl.ds(halo_row(d), DEEP), pl.ds(edge, 2 * nx)]
         return remote(land, land, h_send.at[d, j], h_recv.at[d, j], {"gy": z_peer(1 - d)})
 
+    apart = lax.broadcasted_iota(jnp.int32, (2, nz, nz), 1) - lax.broadcasted_iota(jnp.int32, (2, nz, nz), 2)
+    apart = jnp.abs(apart).reshape(2 * nz, nz)
+    weights[...] = jnp.where(apart == 1, -16.0, jnp.where(apart == 2, 1.0, 0.0)).astype(jnp.bfloat16)
     zero = jnp.zeros((8, nz), jnp.float32)
     rows_all = ny + 2 * DEEP
 
@@ -466,12 +466,16 @@
                 r = i + halo_row(1 - d)
                 for p in range(parts):
                     for j in range(own):
-                        for ref in (psi, half, t1, t2, t3):
+                        for ref in (psi, half):
                             for x in range(0, 2 * nx, 8):
                                 ref[p, j, r, pl.ds(edge + x, 8)] = zero
                 return 0
 
             lax.fori_loop(0, DEEP, clear_row, 0)
+            for i in range(VDEEP):
+                for x in range(0, 2 * nx, 8):
+                    v_now[i + (0 if d == 0 else ny + VDEEP), pl.ds(x, 8)] = zero
+                    v_next[i + (0 if d == 0 else ny + VDEEP), pl.ds(x, 8)] = zero
 
     give_in.wait()
     keep_in.wait()
@@ -497,6 +501,7 @@
     first.start()
     ext_in.wait()
     first.wait_recv()
+    pl.semaphore_signal(ready, inc=1, device_id={"gx": ox}, device_id_type=MESH)
     my_rows = pl.ds(mid * core, mid)
     chip_sum[...] = dens[my_rows] + chip_in[my_rows]
     second = remote(chip_sum, plane_in, b_send.at[0], b_recv.at[0], {"band": far_gb})
@@ -514,9 +519,11 @@
     todo = [(j, q) for j in range(own) for q in piece_order]
     forward(*todo[0])
     second.wait_recv()
+    pl.semaphore_wait(ready, 1)
     shift = -1.5 * centre_weight
     v_rows = pl.ds(VDEEP + mid * core, mid)
-    v_now[v_rows, here] = ext_all[my_rows, here] - exchange_coef * cube_root(chip_sum[...] + plane_in[...]) + shift
+    mine_now = ext_all[my_rows, here] - exchange_coef * cube_root(chip_sum[...] + plane_in[...])
+    v_now[v_rows, here] = (mine_now + shift) * SCALE
 
     own_slot = v_now.at[v_rows, here]
     to_mate = remote(own_slot, own_slot, c_send.at[0, 0], c_recv.at[0, 0], {"band": mate})
@@ -568,64 +575,71 @@
 
     psi_in.wait()
 
-    lane = lax.broadcasted_iota(jnp.int32, (8, nz), 1)
-    near = -0.5 * near_weight
-    far = -0.5 * far_weight
-    below1 = jnp.where(lane >= 1, near, 0.0)
-    above1 = jnp.where(lane < nz - 1, near, 0.0)
-    below2 = jnp.where(lane >= 2, far, 0.0)
-    above2 = jnp.where(lane < nz - 2, far, 0.0)
-
-    def image(src, v, p, j, r, x):
-        def at(row, col):
-            return src[p, j, row, pl.ds(edge + col, 8)]
-
-        c = at(r, x)
-        one = (at(r, x - 1) + at(r, x + 1)) + (at(r - 1, x) + at(r + 1, x))
-        two = (at(r, x - 2) + at(r, x + 2)) + (at(r - 2, x) + at(r + 2, x))
-        total = v * c + near * one + far * two
-        total = total + pltpu.roll(c, 1, 1) * below1 + pltpu.roll(c, nz - 1, 1) * above1
-        return total + (pltpu.roll(c, 2, 1) * below2 + pltpu.roll(c, nz - 2, 1) * above2)
-
     cols = range(0, 2 * nx, 8)
-
-    def level(src, dst, pot, j, first_row, count):
-        for i in range(count):
-            r = first_row + i
+    inside = [has[d].astype(jnp.float32) for d in (0, 1)]
+    group = 4
+
+    def images(src, pot, j, first_row, emit):
+        centres, lhs = {}, []
+        for r in range(first_row, first_row + group):
+            for p in range(parts):
+                c = src[p, j, r, pl.ds(edge, 2 * nx)]
+                top = c.astype(jnp.bfloat16)
+                rest = (c - top.astype(jnp.float32)).astype(jnp.bfloat16)
+                centres[r, p] = c, 2 * nx * len(lhs)
+                lhs.append(jnp.concatenate([top, rest], axis=1))
+        lines = jnp.dot(jnp.concatenate(lhs, axis=0), weights[...], preferred_element_type=jnp.float32)
+        for r in range(first_row, first_row + group):
             for x in cols:
                 v = pot[r - DEEP + VDEEP, pl.ds(x, 8)]
+                values = []
                 for p in range(parts):
-                    dst[p, j, r, pl.ds(edge + x, 8)] = image(src, v, p, j, r, x)
-
-    def rows_of(src, dst, pot, j, first_row, count, group):
-        def some(i, _):
-            level(src, dst, pot, j, first_row + i * group, group)
-            return 0
-
-        lax.fori_loop(0, count // group, some, 0)
-
-    def chain(start, pot, j):
-        for src, dst, deep in ((start, t1, 6), (t1, t2, 4), (t2, t3, 2)):
-            for side in (0, 1):
-
-                @pl.when(has[side])
-                def _():
-                    rows_of(src, dst, pot, j, DEEP + ny if side else DEEP - deep, deep, 2)
-
-            rows_of(src, dst, pot, j, DEEP, ny, 4)
-
-    def last(start, pot, j, r, x, act):
-        v = pot[r - DEEP + VDEEP, pl.ds(x, 8)]
-        ts = [[t[p, j, r, pl.ds(edge + x, 8)] for t in (start, t1, t2, t3)] for p in range(parts)]
-        for p in range(parts):
-            ts[p].append(image(t3, v, p, j, r, x))
-
-        def combine(s):
-            even = [ts[p][0] + (-(s**2) / 2) * ts[p][2] + (s**4 / 24) * ts[p][4] for p in range(2)]
-            odd = [s * ts[p][1] + (-(s**3) / 6) * ts[p][3] for p in range(2)]
-            return even[0] + odd[1], even[1] - odd[0]
-
-        act(combine)
+
+                    def at(row, col):
+                        return src[p, j, row, pl.ds(edge + col, 8)]
+
+                    c, place = centres[r, p]
+                    one = (at(r, x - 1) + at(r, x + 1)) + (at(r - 1, x) + at(r + 1, x))
+                    two = (at(r, x - 2) + at(r, x + 2)) + (at(r - 2, x) + at(r + 2, x))
+                    line = lines[place + x : place + x + 8]
+                    value = v * c[x : x + 8] + ((two - 16.0 * one) + line)
+                    if r < DEEP:
+                        value = value * inside[0]
+                    if r >= DEEP + ny:
+                        value = value * inside[1]
+                    values.append(value)
+                emit(r, x, values)
+
+    def exponential(start, pot, j, act, after):
+        terms = (start, t1, t2, t3)
+
+        def store(dst):
+            def emit(r, x, values):
+                for p, value in enumerate(values):
+                    dst[p, j, r, pl.ds(edge + x, 8)] = value
+
+            return emit
+
+        def finish(r, x, values):
+            ts = [[t[p, j, r, pl.ds(edge + x, 8)] for t in terms] + [values[p]] for p in range(parts)]
+
+            def combine(s):
+                u = s / SCALE
+                even = [ts[p][0] + (-(u**2) / 2) * ts[p][2] + (u**4 / 24) * ts[p][4] for p in range(2)]
+                odd = [u * ts[p][1] + (-(u**3) / 6) * ts[p][3] for p in range(2)]
+                return even[0] + odd[1], even[1] - odd[0]
+
+            act(r - DEEP, x, combine)
+
+        emits = [store(t1), store(t2), store(t3), finish]
+        for g in range((ny + 12) // group + 3):
+            for k, emit in enumerate(emits):
+                deep = 6 - 2 * k
+                i = g - k
+                if 0 <= i < (ny + 2 * deep) // group:
+                    images(terms[k], pot, j, DEEP - deep + group * i, emit)
+                    if k == 3:
+                        after(i)
 
     for j in range(own):
         for side in (0, 1):
@@ -637,27 +651,16 @@
                 for q in goes[d]:
                     f_land(j, d, q).wait_recv()
 
-        chain(psi, v_now, j)
-
-        def finish_row(i, _):
-            for k in range(2):
-                y = 2 * i + k
-                r = DEEP + y
-                for x in cols:
-
-                    def act(combine):
-                        for p, value in enumerate(combine(step_length / 2)):
-                            half[p, j, r, pl.ds(edge + x, 8)] = value
-                        a, b = combine(step_length)
-                        square = a * a + b * b
-                        if j:
-                            square = square + partial[y, pl.ds(x, 8)]
-                        partial[y, pl.ds(x, 8)] = square
-
-                    last(psi, v_now, j, r, x, act)
-            return 0
-
-        lax.fori_loop(0, ny // 2, finish_row, 0)
+        def keep_both(y, x, combine):
+            for p, value in enumerate(combine(step_length / 2)):
+                half[p, j, DEEP + y, pl.ds(edge + x, 8)] = value
+            re, im = combine(step_length)
+            square = re * re + im * im
+            if j:
+                square = square + partial[y, pl.ds(x, 8)]
+            partial[y, pl.ds(x, 8)] = square
+
+        exponential(psi, v_now, j, keep_both, lambda i: None)
         if j == own - 1:
             mine = pl.ds(pl.multiple_of(nx * core, nx), nx)
             theirs = pl.ds(pl.multiple_of(nx * (1 - core), nx), nx)
@@ -681,7 +684,8 @@
     for copy in spread:
         copy.wait_recv()
     total = (done[...] + pieces_in[0]) + (pieces_in[1] + pieces_in[2])
-    v_next[pl.ds(VDEEP, ny), mine] = ext_all[:, mine] - exchange_coef * cube_root(total) + shift
+    mine_next = ext_all[:, mine] - exchange_coef * cube_root(total)
+    v_next[pl.ds(VDEEP, ny), mine] = (mine_next + shift) * SCALE
     next_z = []
     for d in (0, 1):
         z_src = v_next.at[pl.ds(ny if d else VDEEP, VDEEP), mine]
@@ -701,7 +705,7 @@
     next_mate = remote(whole, whole, c_send.at[1, 0], c_recv.at[1, 0], {"band": mate})
     next_mate.start()
     v_wait(v_next, 1, 0, pl.ds(VDEEP, ny), theirs)
-    pot_ref[...] = v_next[pl.ds(VDEEP, ny), here] - shift
+    pot_ref[...] = v_next[pl.ds(VDEEP, ny), here] * (1.0 / SCALE) - shift
     for side in (0, 1):
 
         @pl.when(has[side])
@@ -734,19 +738,15 @@
             def _():
                 h_land(j, 1 - side).wait_recv()
 
-        chain(half, v_next, j)
-        for q in pieces:
-            for k in range(quarter):
-                y = quarter * q + k
-                for x in cols:
-
-                    def act(combine):
-                        for p, value in enumerate(combine(step_length / 2)):
-                            result[p, j, y, pl.ds(x, 8)] = value
-
-                    last(half, v_next, j, DEEP + y, x, act)
+        def keep_result(y, x, combine):
+            for p, value in enumerate(combine(step_length / 2)):
+                result[p, j, y, pl.ds(x, 8)] = value
+
+        def send_back(q):
             back_copy(j, q).start()
             stay_copy(j, q).start()
+
+        exponential(half, v_next, j, keep_result, send_back)
 
     first.wait_send()
     second.wait_send()
@@ -810,6 +810,7 @@
             pltpu.VMEM((3, ny, nx, nz), jnp.float32),
             block,
             pltpu.VMEM((parts, own, ny, 2 * nx, nz), jnp.float32),
+            pltpu.VMEM((2 * nz, nz), jnp.bfloat16),
             dma((4,)),
             dma((own, nq)), dma((own, nq)),
             dma((2, own)), dma((2, own)),
@@ -821,11 +822,15 @@
             dma((1,)), dma((1,)),
             dma((own, nq)), dma((own, nq)),
             dma((own, nq)),
+            pltpu.SemaphoreType.REGULAR,
         ],
         compiler_params=pltpu.CompilerParams(
-            collective_id=0, has_side_effects=True, vmem_limit_bytes=60 * 1024 * 1024
+            collective_id=0, has_side_effects=True, vmem_limit_bytes=32 * 1024 * 1024
         ),
-    )(jnp.transpose(orbitals, (0, 1, 3, 2, 4)), jnp.swapaxes(external, 0, 1))
+    )(
+        pltpu.with_memory_space_constraint(jnp.transpose(orbitals, (0, 1, 3, 2, 4)), pltpu.HBM),
+        pltpu.with_memory_space_constraint(jnp.swapaxes(external, 0, 1), pltpu.HBM),
+    )
     return jnp.transpose(result, (0, 1, 3, 2, 4)), jnp.swapaxes(potential, 0, 1)
 
 

time: 41.7 us -> 33.5 us (0.80)
  Pallas kernels: 38.5 us -> 31.3 us
  local copies, waits for them, and re-layouts: 2.41 us -> 1.37 us
    pallas_call x1, Pallas kernels: 38.5 us -> 31.3 us  [whole_body(): pl.pallas_call(functools.partial(whole_kernel, counts), out_shape=(jax.Sh...]
    unnamed x4 -> x2, local copies, waits for them, and re-layouts: 2.41 us -> 1.37 us
where the time goes in v2:
time: 33.5 us; the launch traced here: 33.4 us
  Pallas kernels  31.3 us (93%)
  local copies, waits for them, and re-layouts  1.37 us (4%)
  between operations  0.64 us (2%)
    pallas_call x1, Pallas kernels, whole_body(): pl.pallas_call(functools.partial(whole_kernel, counts), out_shape=(jax.Sh...  31.3 us
    unnamed x2, local copies, waits for them, and re-layouts  1.37 us

profile of v2, /device:TPU:0, one launch (start us, length us, event | category | flops | bytes accessed | tf_op | source)
XLA Modules:
  0.0 33.4 jit_solution(1407072926016366031)
XLA Ops:
  0.6 31.3 %shard_map.41 = (f32[2,4,12,8,128]{4,3,2,1,0:T(8,128)S(1)}, f32[12,8,128]{2,1,0:T(8,128)S(1)}) custom-call(f32[2,4,12,8,128]{4,3,2,1,0:T(8,128)} %bitcast.6, f32[12,8,128]{2,1,0:T(8,128)} %bitcast.7), custom_call_target="tpu_custom_call" | custom-call | tf_op jit(solution)/shard_map/pallas_call | solution.py:794
  32.0 0.7 %copy.6 = f32[2,4,8,12,128]{4,2,3,1,0:T(8,128)} copy(f32[2,4,8,12,128]{4,2,3,1,0:T(8,128)S(1)} %bitcast.4) | data formatting | bytes 786432
  32.7 0.6 %copy.7 = f32[8,12,128]{2,0,1:T(8,128)} copy(f32[8,12,128]{2,0,1:T(8,128)S(1)} %bitcast.5) | data formatting | bytes 98304

commit v3 on v2

--- a/solution.py
+++ b/solution.py
@@ -334,8 +334,9 @@
 def whole_kernel(counts, orb_hbm, ext_hbm, out_ref, pot_ref, *scratch):
     (
         psi, half, t1, t2, t3, orb_v, ext_all, v_now, v_next, dens, chip_in, chip_sum, plane_in, partial, swap_in,
-        pieces_in, done, result, weights, in_sem, x_send, x_recv, z_send, z_recv, f_send, f_recv, h_send, h_recv,
-        a_send, a_recv, b_send, b_recv, c_send, c_recv, e_send, e_recv, r_send, r_recv, l_sem, ready,
+        pieces_in, done, result, pot_v, weights, in_sem, x_send, x_recv, z_send, z_recv, f_send, f_recv, h_send, h_recv,
+        a_send, a_recv, b_send, b_recv, c_send, c_recv, e_send, e_recv, r_send, r_recv, l_sem,
+        s_send, s_recv, p_send, p_recv, v_send, v_recv, m_send, m_recv, ready,
     ) = scratch
     n_x, n_y, n_b = counts
     parts, nb, ny, nx, nz = orb_hbm.shape
@@ -554,7 +555,6 @@
     to_mate.start()
     ext_here, ext_there = ext_all.at[:, here], ext_all.at[:, there]
     ext_over = remote(ext_here, ext_here, e_send.at[0], e_recv.at[0], {"gx": ox})
-    ext_over.start()
     for pair in todo[1:]:
         forward(*pair)
 
@@ -574,6 +574,7 @@
             v_wait(v_now, 0, 4 + 2 * side, rows, there)
 
     psi_in.wait()
+    ext_over.start()
 
     cols = range(0, 2 * nx, 8)
     inside = [has[d].astype(jnp.float32) for d in (0, 1)]
@@ -641,6 +642,44 @@
                     if k == 3:
                         after(i)
 
+    mine = pl.ds(pl.multiple_of(nx * core, nx), nx)
+    theirs = pl.ds(pl.multiple_of(nx * (1 - core), nx), nx)
+
+    def swap_copy(q):
+        rows = pl.ds(quarter * q, quarter)
+        return remote(partial.at[rows, theirs], swap_in.at[rows], s_send.at[q], s_recv.at[q], {"band": mate})
+
+    def spread_copy(q, n):
+        rows = pl.ds(quarter * q, quarter)
+        peer = ({"gx": ox, "band": far_gb}, {"gx": ox}, {"band": far_gb})[n]
+        return remote(done.at[rows], pieces_in.at[n, rows], p_send.at[q, n], p_recv.at[q, n], peer)
+
+    def halo_span(q, d):
+        low, high = (ny - VDEEP, ny) if d else (0, VDEEP)
+        return max(low, quarter * q), min(high, quarter * (q + 1))
+
+    def v_halo_out(q, d):
+        copies = []
+        for n, b in enumerate((gb, mate)):
+            low, high = halo_span(q, d)
+            src = v_next.at[pl.ds(VDEEP + low, high - low), mine]
+            dst = v_next.at[pl.ds(VDEEP + low + (-ny if d else ny), high - low), mine]
+            copies.append(
+                remote(src, dst, v_send.at[q, d, n], v_recv.at[q, d, core], {"gy": z_peer(d), "band": b})
+            )
+        return copies
+
+    def v_halo_land(q, d, c):
+        low, high = halo_span(q, d)
+        land = v_next.at[pl.ds(VDEEP + low + (-ny if d else ny), high - low), pl.ds(nx * c, nx)]
+        return remote(land, land, v_send.at[q, d, c], v_recv.at[q, d, c], {"gy": z_peer(1 - d)})
+
+    spans = [[q for q in pieces if halo_span(q, d)[0] < halo_span(q, d)[1]] for d in (0, 1)]
+
+    def v_mate(q, tile):
+        rows = v_next.at[pl.ds(VDEEP + quarter * q, quarter), tile]
+        return remote(rows, rows, m_send.at[q], m_recv.at[q], {"band": mate})
+
     for j in range(own):
         for side in (0, 1):
 
@@ -660,60 +699,53 @@
                 square = square + partial[y, pl.ds(x, 8)]
             partial[y, pl.ds(x, 8)] = square
 
-        exponential(psi, v_now, j, keep_both, lambda i: None)
-        if j == own - 1:
-            mine = pl.ds(pl.multiple_of(nx * core, nx), nx)
-            theirs = pl.ds(pl.multiple_of(nx * (1 - core), nx), nx)
-            third = remote(partial.at[:, theirs], swap_in, a_send.at[1], a_recv.at[1], {"band": mate})
-            third.start()
+        def swap(i):
+            if j == own - 1:
+                swap_copy(i).start()
+
+        exponential(psi, v_now, j, keep_both, swap)
         for d in (0, 1):
 
             @pl.when(has[d])
             def _():
                 h_copy(j, d).start()
 
-    third.wait_recv()
-    done[...] = partial[:, mine] + swap_in[...]
-    spread = [
-        remote(done, pieces_in.at[n], b_send.at[1 + n], b_recv.at[1 + n], peer)
-        for n, peer in enumerate(({"gx": ox}, {"band": far_gb}, {"gx": ox, "band": far_gb}))
-    ]
-    for copy in (spread[2], spread[0], spread[1]):
-        copy.start()
+    for q in pieces:
+        rows = pl.ds(quarter * q, quarter)
+        swap_copy(q).wait_recv()
+        done[rows] = partial[rows, mine] + swap_in[rows]
+        for n in range(3):
+            spread_copy(q, n).start()
     remote(ext_there, ext_there, e_send.at[0], e_recv.at[0], {"gx": ox}).wait_recv()
-    for copy in spread:
-        copy.wait_recv()
-    total = (done[...] + pieces_in[0]) + (pieces_in[1] + pieces_in[2])
-    mine_next = ext_all[:, mine] - exchange_coef * cube_root(total)
-    v_next[pl.ds(VDEEP, ny), mine] = (mine_next + shift) * SCALE
-    next_z = []
-    for d in (0, 1):
-        z_src = v_next.at[pl.ds(ny if d else VDEEP, VDEEP), mine]
-        z_dst = v_next.at[pl.ds(0 if d else ny + VDEEP, VDEEP), mine]
-        copies = [
-            remote(z_src, z_dst, c_send.at[1, 1 + 2 * d + n], c_recv.at[1, 1 + 2 * d + core], {"gy": z_peer(d), "band": b})
-            for n, b in enumerate((gb, mate))
-        ]
-        next_z.append(copies)
-
-        @pl.when(has[d])
-        def _():
-            for copy in copies:
-                copy.start()
-
-    whole = v_next.at[pl.ds(VDEEP, ny), mine]
-    next_mate = remote(whole, whole, c_send.at[1, 0], c_recv.at[1, 0], {"band": mate})
-    next_mate.start()
-    v_wait(v_next, 1, 0, pl.ds(VDEEP, ny), theirs)
-    pot_ref[...] = v_next[pl.ds(VDEEP, ny), here] * (1.0 / SCALE) - shift
+    for q in pieces:
+        rows = pl.ds(quarter * q, quarter)
+        for n in range(3):
+            spread_copy(q, n).wait_recv()
+        total = (done[rows] + pieces_in[0, rows]) + (pieces_in[1, rows] + pieces_in[2, rows])
+        mine_next = ext_all[rows, mine] - exchange_coef * cube_root(total)
+        v_next[pl.ds(VDEEP + quarter * q, quarter), mine] = (mine_next + shift) * SCALE
+        for d in (0, 1):
+            if q in spans[d]:
+
+                @pl.when(has[d])
+                def _():
+                    for copy in v_halo_out(q, d):
+                        copy.start()
+
+        v_mate(q, mine).start()
+    for q in pieces:
+        v_mate(q, theirs).wait_recv()
+    pot_v[...] = v_next[pl.ds(VDEEP, ny), here] * (1.0 / SCALE) - shift
+    pot_out = pltpu.make_async_copy(pot_v, pot_ref, in_sem.at[4])
+    pot_out.start()
     for side in (0, 1):
 
         @pl.when(has[side])
         def _():
             d = 1 - side
-            rows = pl.ds(side * (ny + VDEEP), VDEEP)
-            for c in (0, 1):
-                v_wait(v_next, 1, 1 + 2 * d + c, rows, pl.ds(nx * c, nx))
+            for q in spans[d]:
+                for c in (0, 1):
+                    v_halo_land(q, d, c).wait_recv()
 
     def back_copy(j, q):
         rows = pl.ds(quarter * q, quarter)
@@ -748,13 +780,17 @@
 
         exponential(half, v_next, j, keep_result, send_back)
 
+    pot_out.wait()
     first.wait_send()
     second.wait_send()
-    third.wait_send()
     to_mate.wait_send()
     ext_over.wait_send()
-    next_mate.wait_send()
-    for copy in to_x + spread:
+    for q in pieces:
+        swap_copy(q).wait_send()
+        v_mate(q, mine).wait_send()
+        for n in range(3):
+            spread_copy(q, n).wait_send()
+    for copy in to_x:
         copy.wait_send()
 
     @pl.when(z_ok)
@@ -766,8 +802,9 @@
 
         @pl.when(has[d])
         def _():
-            for copy in next_z[d]:
-                copy.wait_send()
+            for q in spans[d]:
+                for copy in v_halo_out(q, d):
+                    copy.wait_send()
             for j in range(own):
                 z_copy(j, d).wait_send()
                 h_copy(j, d).wait_send()
@@ -798,7 +835,7 @@
             jax.ShapeDtypeStruct((ny, nx, nz), jnp.float32),
         ),
         in_specs=[pl.BlockSpec(memory_space=pltpu.HBM)] * 2,
-        out_specs=(pl.BlockSpec(memory_space=pltpu.VMEM),) * 2,
+        out_specs=(pl.BlockSpec(memory_space=pl.ANY),) * 2,
         scratch_shapes=[
             term, term, term, term, term,
             pltpu.VMEM((parts, nb, ny, nx, nz), jnp.float32),
@@ -810,18 +847,23 @@
             pltpu.VMEM((3, ny, nx, nz), jnp.float32),
             block,
             pltpu.VMEM((parts, own, ny, 2 * nx, nz), jnp.float32),
+            block,
             pltpu.VMEM((2 * nz, nz), jnp.bfloat16),
-            dma((4,)),
+            dma((5,)),
             dma((own, nq)), dma((own, nq)),
             dma((2, own)), dma((2, own)),
             dma((2, own, nq)), dma((2, own, nq)),
             dma((2, own)), dma((2, own)),
-            dma((2,)), dma((2,)),
-            dma((4,)), dma((4,)),
-            dma((2, 7)), dma((2, 7)),
+            dma((1,)), dma((1,)),
+            dma((1,)), dma((1,)),
+            dma((1, 7)), dma((1, 7)),
             dma((1,)), dma((1,)),
             dma((own, nq)), dma((own, nq)),
             dma((own, nq)),
+            dma((nq,)), dma((nq,)),
+            dma((nq, 3)), dma((nq, 3)),
+            dma((nq, 2, 2)), dma((nq, 2, 2)),
+            dma((nq,)), dma((nq,)),
             pltpu.SemaphoreType.REGULAR,
         ],
         compiler_params=pltpu.CompilerParams(

time: 33.5 us -> 32.7 us (0.976)
  Pallas kernels: 31.3 us -> 30.6 us
    pallas_call x1, Pallas kernels: 31.3 us -> 30.6 us  [whole_body(): pl.pallas_call(functools.partial(whole_kernel, counts), out_shape=(jax.Sh...]
where the time goes in v3:
time: 32.7 us; the launch traced here: 32.6 us
  Pallas kernels  30.6 us (94%)
  local copies, waits for them, and re-layouts  1.37 us (4%)
  between operations  0.64 us (2%)
    pallas_call x1, Pallas kernels, whole_body(): pl.pallas_call(functools.partial(whole_kernel, counts), out_shape=(jax.Sh...  30.6 us
    unnamed x2, local copies, waits for them, and re-layouts  1.37 us

profile of v3, /device:TPU:0, one launch (start us, length us, event | category | flops | bytes accessed | tf_op | source)
XLA Modules:
  0.0 32.6 jit_solution(4648530973344072026)
XLA Ops:
  0.6 30.6 %shard_map.41 = (f32[2,4,12,8,128]{4,3,2,1,0:T(8,128)S(1)}, f32[12,8,128]{2,1,0:T(8,128)S(1)}) custom-call(f32[2,4,12,8,128]{4,3,2,1,0:T(8,128)} %bitcast.6, f32[12,8,128]{2,1,0:T(8,128)} %bitcast.7), custom_call_target="tpu_custom_call" | custom-call | tf_op jit(solution)/shard_map/pallas_call | solution.py:831
  31.2 0.7 %copy.6 = f32[2,4,8,12,128]{4,2,3,1,0:T(8,128)} copy(f32[2,4,8,12,128]{4,2,3,1,0:T(8,128)S(1)} %bitcast.4) | data formatting | bytes 786432
  31.9 0.6 %copy.7 = f32[8,12,128]{2,0,1:T(8,128)} copy(f32[8,12,128]{2,0,1:T(8,128)S(1)} %bitcast.5) | data formatting | bytes 98304

commit v4 on v3

--- a/solution.py
+++ b/solution.py
@@ -334,9 +334,10 @@
 def whole_kernel(counts, orb_hbm, ext_hbm, out_ref, pot_ref, *scratch):
     (
         psi, half, t1, t2, t3, orb_v, ext_all, v_now, v_next, dens, chip_in, chip_sum, plane_in, partial, swap_in,
-        pieces_in, done, result, pot_v, weights, in_sem, x_send, x_recv, z_send, z_recv, f_send, f_recv, h_send, h_recv,
-        a_send, a_recv, b_send, b_recv, c_send, c_recv, e_send, e_recv, r_send, r_recv, l_sem,
-        s_send, s_recv, p_send, p_recv, v_send, v_recv, m_send, m_recv, ready,
+        pieces_in, done, result, pot_v, weights,
+        in_sem, row_send, block_send, half_send, side_send, v_now_send, v_next_send, stay_sem,
+        x_recv, halo_recv, half_recv, first_recv, second_recv, mate_recv, over_recv, v_side_recv,
+        ext_recv, swap_recv, spread_recv, v_next_recv, back_recv, ready,
     ) = scratch
     n_x, n_y, n_b = counts
     parts, nb, ny, nx, nz = orb_hbm.shape
@@ -389,6 +390,12 @@
             src_ref=src, dst_ref=dst, send_sem=send, recv_sem=recv, device_id=peer, device_id_type=MESH
         )
 
+    def sent(like, sem):
+        remote(like, like, sem, sem, {"band": mate}).wait_send()
+
+    def landed(like, sem):
+        remote(like, like, sem, sem, {"band": mate}).wait_recv()
+
     quarter = 4
     pieces = list(range(ny // quarter))
     goes = ([q for q in pieces if quarter * q < DEEP], [q for q in pieces if quarter * q >= ny - DEEP])
@@ -398,12 +405,12 @@
         return remote(
             orb_v.at[:, own * ox + j, pl.ds(quarter * q, quarter)],
             psi.at[:, j, pl.ds(DEEP + quarter * q, quarter), here_pad],
-            x_send.at[j, q], x_recv.at[j, q], {"gx": ox},
+            row_send, x_recv.at[j, q], {"gx": ox},
         )
 
     def x_land(j, q):
         land = psi.at[:, j, pl.ds(DEEP + quarter * q, quarter), there_pad]
-        return remote(land, land, x_send.at[j, q], x_recv.at[j, q], {"gx": ox})
+        return remote(land, land, row_send, x_recv.at[j, q], {"gx": ox})
 
     def halo_row(d):
         return 0 if d else DEEP + ny
@@ -412,12 +419,11 @@
         return remote(
             orb_v.at[:, own * gx + j, pl.ds(ny - DEEP if d else 0, DEEP)],
             psi.at[:, j, pl.ds(halo_row(d), DEEP), here_pad],
-            z_send.at[d, j], z_recv.at[d, j], {"gy": z_peer(d)},
-        )
-
-    def z_land(j, d):
-        land = psi.at[:, j, pl.ds(halo_row(d), DEEP), here_pad]
-        return remote(land, land, z_send.at[d, j], z_recv.at[d, j], {"gy": z_peer(1 - d)})
+            side_send.at[d], halo_recv.at[d, j], {"gy": z_peer(d)},
+        )
+
+    def halo_land(ref, j, d, sems):
+        landed(ref.at[:, j, pl.ds(halo_row(d), DEEP), pl.ds(edge, 2 * nx)], sems.at[d, j])
 
     def f_row(d, q):
         return DEEP + quarter * q + (-ny if d else ny)
@@ -426,23 +432,15 @@
         return remote(
             psi.at[:, j, pl.ds(DEEP + quarter * q, quarter), there_pad],
             psi.at[:, j, pl.ds(f_row(d, q), quarter), there_pad],
-            f_send.at[d, j, q], f_recv.at[d, j, q], {"gy": z_peer(d)},
-        )
-
-    def f_land(j, d, q):
-        land = psi.at[:, j, pl.ds(f_row(d, q), quarter), there_pad]
-        return remote(land, land, f_send.at[d, j, q], f_recv.at[d, j, q], {"gy": z_peer(1 - d)})
+            side_send.at[d], halo_recv.at[d, j], {"gy": z_peer(d)},
+        )
 
     def h_copy(j, d):
         return remote(
             half.at[:, j, pl.ds(ny if d else DEEP, DEEP), pl.ds(edge, 2 * nx)],
             half.at[:, j, pl.ds(halo_row(d), DEEP), pl.ds(edge, 2 * nx)],
-            h_send.at[d, j], h_recv.at[d, j], {"gy": z_peer(d)},
-        )
-
-    def h_land(j, d):
-        land = half.at[:, j, pl.ds(halo_row(d), DEEP), pl.ds(edge, 2 * nx)]
-        return remote(land, land, h_send.at[d, j], h_recv.at[d, j], {"gy": z_peer(1 - d)})
+            side_send.at[d], half_recv.at[d, j], {"gy": z_peer(d)},
+        )
 
     apart = lax.broadcasted_iota(jnp.int32, (2, nz, nz), 1) - lax.broadcasted_iota(jnp.int32, (2, nz, nz), 2)
     apart = jnp.abs(apart).reshape(2 * nz, nz)
@@ -498,14 +496,14 @@
                 v = orb_v[p, j, y]
                 total = v * v if total is None else total + v * v
         dens[y] = total
-    first = remote(dens, chip_in, a_send.at[0], a_recv.at[0], {"band": mate})
+    first = remote(dens, chip_in, block_send, first_recv, {"band": mate})
     first.start()
     ext_in.wait()
     first.wait_recv()
     pl.semaphore_signal(ready, inc=1, device_id={"gx": ox}, device_id_type=MESH)
     my_rows = pl.ds(mid * core, mid)
     chip_sum[...] = dens[my_rows] + chip_in[my_rows]
-    second = remote(chip_sum, plane_in, b_send.at[0], b_recv.at[0], {"band": far_gb})
+    second = remote(chip_sum, plane_in, half_send, second_recv, {"band": far_gb})
     second.start()
 
     def forward(j, q):
@@ -527,9 +525,9 @@
     v_now[v_rows, here] = (mine_now + shift) * SCALE
 
     own_slot = v_now.at[v_rows, here]
-    to_mate = remote(own_slot, own_slot, c_send.at[0, 0], c_recv.at[0, 0], {"band": mate})
+    to_mate = remote(own_slot, own_slot, half_send, mate_recv, {"band": mate})
     to_x = [
-        remote(own_slot, own_slot, c_send.at[0, 1 + n], c_recv.at[0, 1 + core], {"gx": ox, "band": b})
+        remote(own_slot, own_slot, block_send, over_recv, {"gx": ox, "band": b})
         for n, b in enumerate((gb, mate))
     ]
     z_src = v_now.at[pl.ds(VDEEP + core * (ny - VDEEP), VDEEP), here]
@@ -538,7 +536,7 @@
     z_ok = jnp.logical_and(z_to >= 0, z_to < n_y)
     to_z = [
         remote(
-            z_src, z_dst, c_send.at[0, 3 + 2 * m + n], c_recv.at[0, 5 - 2 * core + m],
+            z_src, z_dst, v_now_send, v_side_recv.at[1 - core],
             {"gx": x, "gy": z_to, "band": b},
         )
         for m, x in enumerate((gx, ox))
@@ -554,24 +552,17 @@
 
     to_mate.start()
     ext_here, ext_there = ext_all.at[:, here], ext_all.at[:, there]
-    ext_over = remote(ext_here, ext_here, e_send.at[0], e_recv.at[0], {"gx": ox})
+    ext_over = remote(ext_here, ext_here, block_send, ext_recv, {"gx": ox})
     for pair in todo[1:]:
         forward(*pair)
 
-    def v_wait(ref, which, slot, rows, cols):
-        land = ref.at[rows, cols]
-        remote(land, land, c_send.at[which, slot], c_recv.at[which, slot], {"band": mate}).wait_recv()
-
-    v_wait(v_now, 0, 0, pl.ds(VDEEP + mid * (1 - core), mid), here)
-    for c in (0, 1):
-        v_wait(v_now, 0, 1 + c, pl.ds(VDEEP + mid * c, mid), there)
+    landed(v_now.at[pl.ds(VDEEP + mid * (1 - core), mid), here], mate_recv)
+    landed(v_now.at[pl.ds(VDEEP, ny), there], over_recv)
     for side in (0, 1):
 
         @pl.when(has[side])
         def _():
-            rows = pl.ds(side * (ny + VDEEP), VDEEP)
-            v_wait(v_now, 0, 3 + 2 * side, rows, here)
-            v_wait(v_now, 0, 4 + 2 * side, rows, there)
+            landed(v_now.at[pl.ds(side * (ny + VDEEP), VDEEP)], v_side_recv.at[side])
 
     psi_in.wait()
     ext_over.start()
@@ -647,12 +638,12 @@
 
     def swap_copy(q):
         rows = pl.ds(quarter * q, quarter)
-        return remote(partial.at[rows, theirs], swap_in.at[rows], s_send.at[q], s_recv.at[q], {"band": mate})
+        return remote(partial.at[rows, theirs], swap_in.at[rows], block_send, swap_recv.at[q], {"band": mate})
 
     def spread_copy(q, n):
         rows = pl.ds(quarter * q, quarter)
         peer = ({"gx": ox, "band": far_gb}, {"gx": ox}, {"band": far_gb})[n]
-        return remote(done.at[rows], pieces_in.at[n, rows], p_send.at[q, n], p_recv.at[q, n], peer)
+        return remote(done.at[rows], pieces_in.at[n, rows], block_send, spread_recv.at[q], peer)
 
     def halo_span(q, d):
         low, high = (ny - VDEEP, ny) if d else (0, VDEEP)
@@ -665,30 +656,22 @@
             src = v_next.at[pl.ds(VDEEP + low, high - low), mine]
             dst = v_next.at[pl.ds(VDEEP + low + (-ny if d else ny), high - low), mine]
             copies.append(
-                remote(src, dst, v_send.at[q, d, n], v_recv.at[q, d, core], {"gy": z_peer(d), "band": b})
+                remote(src, dst, v_next_send.at[d], v_next_recv.at[1 - d], {"gy": z_peer(d), "band": b})
             )
         return copies
 
-    def v_halo_land(q, d, c):
-        low, high = halo_span(q, d)
-        land = v_next.at[pl.ds(VDEEP + low + (-ny if d else ny), high - low), pl.ds(nx * c, nx)]
-        return remote(land, land, v_send.at[q, d, c], v_recv.at[q, d, c], {"gy": z_peer(1 - d)})
-
     spans = [[q for q in pieces if halo_span(q, d)[0] < halo_span(q, d)[1]] for d in (0, 1)]
 
     def v_mate(q, tile):
         rows = v_next.at[pl.ds(VDEEP + quarter * q, quarter), tile]
-        return remote(rows, rows, m_send.at[q], m_recv.at[q], {"band": mate})
+        return remote(rows, rows, block_send, mate_recv, {"band": mate})
 
     for j in range(own):
         for side in (0, 1):
 
             @pl.when(has[side])
             def _():
-                d = 1 - side
-                z_land(j, d).wait_recv()
-                for q in goes[d]:
-                    f_land(j, d, q).wait_recv()
+                halo_land(psi, j, 1 - side, halo_recv)
 
         def keep_both(y, x, combine):
             for p, value in enumerate(combine(step_length / 2)):
@@ -716,11 +699,10 @@
         done[rows] = partial[rows, mine] + swap_in[rows]
         for n in range(3):
             spread_copy(q, n).start()
-    remote(ext_there, ext_there, e_send.at[0], e_recv.at[0], {"gx": ox}).wait_recv()
+    remote(ext_there, ext_there, block_send, ext_recv, {"gx": ox}).wait_recv()
     for q in pieces:
         rows = pl.ds(quarter * q, quarter)
-        for n in range(3):
-            spread_copy(q, n).wait_recv()
+        landed(pieces_in.at[:, rows], spread_recv.at[q])
         total = (done[rows] + pieces_in[0, rows]) + (pieces_in[1, rows] + pieces_in[2, rows])
         mine_next = ext_all[rows, mine] - exchange_coef * cube_root(total)
         v_next[pl.ds(VDEEP + quarter * q, quarter), mine] = (mine_next + shift) * SCALE
@@ -733,8 +715,7 @@
                         copy.start()
 
         v_mate(q, mine).start()
-    for q in pieces:
-        v_mate(q, theirs).wait_recv()
+    landed(v_next.at[pl.ds(VDEEP, ny), theirs], mate_recv)
     pot_v[...] = v_next[pl.ds(VDEEP, ny), here] * (1.0 / SCALE) - shift
     pot_out = pltpu.make_async_copy(pot_v, pot_ref, in_sem.at[4])
     pot_out.start()
@@ -742,33 +723,26 @@
 
         @pl.when(has[side])
         def _():
-            d = 1 - side
-            for q in spans[d]:
-                for c in (0, 1):
-                    v_halo_land(q, d, c).wait_recv()
+            landed(v_next.at[pl.ds(side * (ny + VDEEP), VDEEP)], v_next_recv.at[side])
 
     def back_copy(j, q):
         rows = pl.ds(quarter * q, quarter)
         return remote(
             result.at[:, j, rows, there],
             out_ref.at[:, own * gx + j, rows],
-            r_send.at[j, q], r_recv.at[j, q], {"gx": ox},
-        )
-
-    def back_land(j, q):
-        land = out_ref.at[:, own * ox + j, pl.ds(quarter * q, quarter)]
-        return remote(land, land, r_send.at[j, q], r_recv.at[j, q], {"gx": ox})
+            row_send, back_recv, {"gx": ox},
+        )
 
     def stay_copy(j, q):
         rows = pl.ds(quarter * q, quarter)
-        return pltpu.make_async_copy(result.at[:, j, rows, here], out_ref.at[:, own * gx + j, rows], l_sem.at[j, q])
+        return pltpu.make_async_copy(result.at[:, j, rows, here], out_ref.at[:, own * gx + j, rows], stay_sem)
 
     for j in range(own):
         for side in (0, 1):
 
             @pl.when(has[side])
             def _():
-                h_land(j, 1 - side).wait_recv()
+                halo_land(half, j, 1 - side, half_recv)
 
         def keep_result(y, x, combine):
             for p, value in enumerate(combine(step_length / 2)):
@@ -781,42 +755,23 @@
         exponential(half, v_next, j, keep_result, send_back)
 
     pot_out.wait()
-    first.wait_send()
-    second.wait_send()
-    to_mate.wait_send()
-    ext_over.wait_send()
-    for q in pieces:
-        swap_copy(q).wait_send()
-        v_mate(q, mine).wait_send()
-        for n in range(3):
-            spread_copy(q, n).wait_send()
-    for copy in to_x:
-        copy.wait_send()
+    sent(orb_v, row_send)
+    sent(orb_v, block_send)
+    sent(dens, half_send)
 
     @pl.when(z_ok)
     def _():
-        for copy in to_z:
-            copy.wait_send()
+        sent(v_now.at[pl.ds(0, 2 * VDEEP)], v_now_send)
 
     for d in (0, 1):
 
         @pl.when(has[d])
         def _():
-            for q in spans[d]:
-                for copy in v_halo_out(q, d):
-                    copy.wait_send()
-            for j in range(own):
-                z_copy(j, d).wait_send()
-                h_copy(j, d).wait_send()
-                for q in goes[d]:
-                    f_copy(j, d, q).wait_send()
-
-    for j in range(own):
-        for q in pieces:
-            x_copy(j, q).wait_send()
-            back_copy(j, q).wait_send()
-            stay_copy(j, q).wait()
-            back_land(j, q).wait_recv()
+            sent(v_next.at[pl.ds(0, VDEEP)], v_next_send.at[d])
+            sent(half.at[:, :, pl.ds(0, 2 * DEEP), pl.ds(edge, 2 * nx)], side_send.at[d])
+
+    pltpu.make_async_copy(result.at[..., here, :], out_ref.at[:, keep], stay_sem).wait()
+    landed(out_ref.at[:, give], back_recv)
 
 
 def whole_body(counts, orbitals, external):
@@ -849,21 +804,9 @@
             pltpu.VMEM((parts, own, ny, 2 * nx, nz), jnp.float32),
             block,
             pltpu.VMEM((2 * nz, nz), jnp.bfloat16),
-            dma((5,)),
-            dma((own, nq)), dma((own, nq)),
-            dma((2, own)), dma((2, own)),
-            dma((2, own, nq)), dma((2, own, nq)),
-            dma((2, own)), dma((2, own)),
-            dma((1,)), dma((1,)),
-            dma((1,)), dma((1,)),
-            dma((1, 7)), dma((1, 7)),
-            dma((1,)), dma((1,)),
-            dma((own, nq)), dma((own, nq)),
-            dma((own, nq)),
-            dma((nq,)), dma((nq,)),
-            dma((nq, 3)), dma((nq, 3)),
-            dma((nq, 2, 2)), dma((nq, 2, 2)),
-            dma((nq,)), dma((nq,)),
+            dma((5,)), dma, dma, dma, dma((2,)), dma, dma((2,)), dma,
+            dma((own, nq)), dma((2, own)), dma((2, own)), dma, dma, dma, dma, dma((2,)),
+            dma, dma((nq,)), dma((nq,)), dma((2,)), dma,
             pltpu.SemaphoreType.REGULAR,
         ],
         compiler_params=pltpu.CompilerParams(
@@ -879,7 +822,7 @@
 def body(counts, orbitals, external):
     parts, nb, nx, ny, nz = orbitals.shape
     n_x, n_y, n_b = counts
-    if n_x == 2 and n_b == 4 and nb % 2 == 0 and nx % 8 == 0 and ny % 4 == 0 and ny >= 2 * VDEEP:
+    if n_x == 2 and n_b == 4 and parts * nb == 8 and nx % 8 == 0 and ny % 4 == 0 and ny >= 2 * VDEEP:
         return whole_body(counts, orbitals, external)
     return step_body(counts, orbitals, external)
 

time: 32.7 us -> 31.8 us (0.972)
  Pallas kernels: 30.6 us -> 29.6 us
    pallas_call x1, Pallas kernels: 30.6 us -> 29.6 us  [whole_body(): pl.pallas_call(functools.partial(whole_kernel, counts), out_shape=(jax.Sh...]
where the time goes in v4:
time: 31.8 us; the launch traced here: 31.6 us
  Pallas kernels  29.6 us (93%)
  local copies, waits for them, and re-layouts  1.37 us (4%)
  between operations  0.64 us (2%)
    pallas_call x1, Pallas kernels, whole_body(): pl.pallas_call(functools.partial(whole_kernel, counts), out_shape=(jax.Sh...  29.6 us
    unnamed x2, local copies, waits for them, and re-layouts  1.37 us

profile of v4, /device:TPU:0, one launch (start us, length us, event | category | flops | bytes accessed | tf_op | source)
XLA Modules:
  0.0 31.6 jit_solution(3118495603479973389)
XLA Ops:
  0.6 29.6 %shard_map.41 = (f32[2,4,12,8,128]{4,3,2,1,0:T(8,128)S(1)}, f32[12,8,128]{2,1,0:T(8,128)S(1)}) custom-call(f32[2,4,12,8,128]{4,3,2,1,0:T(8,128)} %bitcast.6, f32[12,8,128]{2,1,0:T(8,128)} %bitcast.7), custom_call_target="tpu_custom_call" | custom-call | tf_op jit(solution)/shard_map/pallas_call | solution.py:786
  30.2 0.7 %copy.6 = f32[2,4,8,12,128]{4,2,3,1,0:T(8,128)} copy(f32[2,4,8,12,128]{4,2,3,1,0:T(8,128)S(1)} %bitcast.4) | data formatting | bytes 786432
  31.0 0.6 %copy.7 = f32[8,12,128]{2,0,1:T(8,128)} copy(f32[8,12,128]{2,0,1:T(8,128)S(1)} %bitcast.5) | data formatting | bytes 98304

commit v5 on v4

--- a/solution.py
+++ b/solution.py
@@ -772,6 +772,17 @@
 
     pltpu.make_async_copy(result.at[..., here, :], out_ref.at[:, keep], stay_sem).wait()
     landed(out_ref.at[:, give], back_recv)
+
+
+def leave(result, potential, result_out, potential_out, sems):
+    copies = [
+        pltpu.make_async_copy(result, result_out, sems.at[0]),
+        pltpu.make_async_copy(potential, potential_out, sems.at[1]),
+    ]
+    for copy in copies:
+        copy.start()
+    for copy in copies:
+        copy.wait()
 
 
 def whole_body(counts, orbitals, external):
@@ -816,6 +827,14 @@
         pltpu.with_memory_space_constraint(jnp.transpose(orbitals, (0, 1, 3, 2, 4)), pltpu.HBM),
         pltpu.with_memory_space_constraint(jnp.swapaxes(external, 0, 1), pltpu.HBM),
     )
+    result, potential = pl.pallas_call(
+        leave,
+        out_shape=tuple(jax.ShapeDtypeStruct(a.shape, a.dtype) for a in (result, potential)),
+        in_specs=[pl.BlockSpec(memory_space=pl.ANY)] * 2,
+        out_specs=(pl.BlockSpec(memory_space=pl.ANY),) * 2,
+        scratch_shapes=[dma((2,))],
+        compiler_params=pltpu.CompilerParams(vmem_limit_bytes=4 * 1024 * 1024),
+    )(result, potential)
     return jnp.transpose(result, (0, 1, 3, 2, 4)), jnp.swapaxes(potential, 0, 1)
 
 

time: 31.8 us -> 31.2 us (0.981)
  local copies, waits for them, and re-layouts: 1.37 us -> 0 us
  Pallas kernels: 29.6 us -> 30.4 us
    unnamed x2 -> x0, local copies, waits for them, and re-layouts: 1.37 us -> none
    pallas_call x0 -> x1, Pallas kernels: none -> 0.77 us  [whole_body(): pl.pallas_call(leave, out_shape=tuple((jax.ShapeDtypeStruct(a.shape, a.dt...]
where the time goes in v5:
time: 31.2 us; the launch traced here: 31 us
  Pallas kernels  30.4 us (97%)
  between operations  0.64 us (2%)
    pallas_call x1, Pallas kernels, whole_body(): pl.pallas_call(functools.partial(whole_kernel, counts), out_shape=(jax.Sh...  29.6 us
    pallas_call x1, Pallas kernels, whole_body(): pl.pallas_call(leave, out_shape=tuple((jax.ShapeDtypeStruct(a.shape, a.dt...  0.77 us

profile of v5, /device:TPU:0, one launch (start us, length us, event | category | flops | bytes accessed | tf_op | source)
XLA Modules:
  0.0 31.0 jit_solution(10888212265403686652)
XLA Ops:
  0.6 29.6 %shard_map.41 = (f32[2,4,12,8,128]{4,3,2,1,0:T(8,128)S(1)}, f32[12,8,128]{2,1,0:T(8,128)S(1)}) custom-call(f32[2,4,12,8,128]{4,3,2,1,0:T(8,128)} %bitcast.4, f32[12,8,128]{2,1,0:T(8,128)} %bitcast.5), custom_call_target="tpu_custom_call" | custom-call | tf_op jit(solution)/shard_map/pallas_call | solution.py:797
  30.2 0.8 %shard_map.42 = (f32[2,4,12,8,128]{4,3,2,1,0:T(8,128)}, f32[12,8,128]{2,1,0:T(8,128)}) custom-call(f32[2,4,12,8,128]{4,3,2,1,0:T(8,128)S(1)} %get-tuple-element.6.result, f32[12,8,128]{2,1,0:T(8,128)S(1)} %get-tuple-element.7.potential), custom_call_target="tpu_custom_call" | custom-call | tf_op jit(solution)/shard_map/pallas_call | solution.py:830

commit v6 on v5

--- a/solution.py
+++ b/solution.py
@@ -334,10 +334,11 @@
 def whole_kernel(counts, orb_hbm, ext_hbm, out_ref, pot_ref, *scratch):
     (
         psi, half, t1, t2, t3, orb_v, ext_all, v_now, v_next, dens, chip_in, chip_sum, plane_in, partial, swap_in,
-        pieces_in, done, result, pot_v, weights,
+        pieces_in, done, result, local_result, pot_v, weights,
         in_sem, row_send, block_send, half_send, side_send, v_now_send, v_next_send, stay_sem,
         x_recv, halo_recv, half_recv, first_recv, second_recv, mate_recv, over_recv, v_side_recv,
-        ext_recv, swap_recv, spread_recv, v_next_recv, back_recv, ready,
+        ext_recv, swap_recv, spread_recv, v_next_recv, back_recv, back_send, share_recv, share_side_send, share_halo_recv,
+        local_sem, ready,
     ) = scratch
     n_x, n_y, n_b = counts
     parts, nb, ny, nx, nz = orb_hbm.shape
@@ -442,6 +443,30 @@
             side_send.at[d], half_recv.at[d, j], {"gy": z_peer(d)},
         )
 
+    shared, guest, lone = 0, own, own - 1
+    data = pl.ds(edge, 2 * nx)
+
+    def share_copy(q):
+        rows = pl.ds(DEEP + quarter * q, quarter)
+        return remote(
+            half.at[:, shared, rows, data], half.at[:, guest, rows, data], row_send, share_recv.at[q], {"gx": ox}
+        )
+
+    def share_rows(q):
+        return half.at[:, guest, pl.ds(DEEP + quarter * q, quarter), data]
+
+    def share_forward(q):
+        rows = share_rows(q)
+        for d in (0, 1):
+            if q in goes[d]:
+
+                @pl.when(has[d])
+                def _():
+                    remote(
+                        rows, half.at[:, guest, pl.ds(f_row(d, q), quarter), data],
+                        share_side_send.at[d], share_halo_recv.at[d], {"gy": z_peer(d)},
+                    ).start()
+
     apart = lax.broadcasted_iota(jnp.int32, (2, nz, nz), 1) - lax.broadcasted_iota(jnp.int32, (2, nz, nz), 2)
     apart = jnp.abs(apart).reshape(2 * nz, nz)
     weights[...] = jnp.where(apart == 1, -16.0, jnp.where(apart == 2, 1.0, 0.0)).astype(jnp.bfloat16)
@@ -450,8 +475,8 @@
 
     def clear(r, _):
         for p in range(parts):
-            for j in range(own):
-                for ref in (psi, half, t1, t2, t3):
+            for ref in (psi, half, t1, t2, t3):
+                for j in range(ref.shape[1]):
                     ref[p, j, r, pl.ds(0, 8)] = zero
                     ref[p, j, r, pl.ds(edge + 2 * nx, 8)] = zero
         return 0
@@ -464,8 +489,8 @@
             def clear_row(i, _):
                 r = i + halo_row(1 - d)
                 for p in range(parts):
-                    for j in range(own):
-                        for ref in (psi, half):
+                    for ref in (psi, half):
+                        for j in range(ref.shape[1]):
                             for x in range(0, 2 * nx, 8):
                                 ref[p, j, r, pl.ds(edge + x, 8)] = zero
                 return 0
@@ -602,7 +627,37 @@
                     values.append(value)
                 emit(r, x, values)
 
-    def exponential(start, pot, j, act, after):
+    def images_here(src, pot, j, first_row, emit):
+        for x in range(0, nx, 8):
+            base = edge + nx * gx + x
+            centres, lhs = {}, []
+            for r in range(first_row, first_row + group):
+                cs = [src[p, j, r, pl.ds(pl.multiple_of(base, 8), 8)] for p in range(parts)]
+                c = jnp.concatenate(cs, axis=0)
+                top = c.astype(jnp.bfloat16)
+                rest = (c - top.astype(jnp.float32)).astype(jnp.bfloat16)
+                centres[r] = cs, 8 * parts * len(lhs)
+                lhs.append(jnp.concatenate([top, rest], axis=1))
+            lines = jnp.dot(jnp.concatenate(lhs, axis=0), weights[...], preferred_element_type=jnp.float32)
+            for r in range(first_row, first_row + group):
+                v = pot[r - DEEP + VDEEP, pl.ds(pl.multiple_of(nx * gx + x, 8), 8)]
+                values = []
+                for p in range(parts):
+
+                    def at(row, col):
+                        return src[p, j, row, pl.ds(base + col, 8)]
+
+                    def by(row):
+                        return src[p, j, row, pl.ds(pl.multiple_of(base, 8), 8)]
+
+                    cs, place = centres[r]
+                    one = (at(r, -1) + at(r, 1)) + (by(r - 1) + by(r + 1))
+                    two = (at(r, -2) + at(r, 2)) + (by(r - 2) + by(r + 2))
+                    line = lines[place + 8 * p : place + 8 * p + 8]
+                    values.append(v * cs[p] + ((two - 16.0 * one) + line))
+                emit(r, x, values)
+
+    def exponential(start, pot, j, act, after, only_here=False):
         terms = (start, t1, t2, t3)
 
         def store(dst):
@@ -613,7 +668,8 @@
             return emit
 
         def finish(r, x, values):
-            ts = [[t[p, j, r, pl.ds(edge + x, 8)] for t in terms] + [values[p]] for p in range(parts)]
+            place = pl.multiple_of(edge + nx * gx + x, 8) if only_here else edge + x
+            ts = [[t[p, j, r, pl.ds(place, 8)] for t in terms] + [values[p]] for p in range(parts)]
 
             def combine(s):
                 u = s / SCALE
@@ -629,7 +685,8 @@
                 deep = 6 - 2 * k
                 i = g - k
                 if 0 <= i < (ny + 2 * deep) // group:
-                    images(terms[k], pot, j, DEEP - deep + group * i, emit)
+                    make = images_here if only_here and k == 3 else images
+                    make(terms[k], pot, j, DEEP - deep + group * i, emit)
                     if k == 3:
                         after(i)
 
@@ -693,12 +750,18 @@
             def _():
                 h_copy(j, d).start()
 
+        if j == shared:
+            share_copy(piece_order[0]).start()
+
     for q in pieces:
         rows = pl.ds(quarter * q, quarter)
         swap_copy(q).wait_recv()
         done[rows] = partial[rows, mine] + swap_in[rows]
         for n in range(3):
             spread_copy(q, n).start()
+    landed(share_rows(piece_order[0]), share_recv.at[piece_order[0]])
+    for q in piece_order[1:]:
+        share_copy(q).start()
     remote(ext_there, ext_there, block_send, ext_recv, {"gx": ox}).wait_recv()
     for q in pieces:
         rows = pl.ds(quarter * q, quarter)
@@ -715,44 +778,53 @@
                         copy.start()
 
         v_mate(q, mine).start()
+    share_forward(piece_order[0])
     landed(v_next.at[pl.ds(VDEEP, ny), theirs], mate_recv)
     pot_v[...] = v_next[pl.ds(VDEEP, ny), here] * (1.0 / SCALE) - shift
     pot_out = pltpu.make_async_copy(pot_v, pot_ref, in_sem.at[4])
     pot_out.start()
+    for q in piece_order[1:]:
+        landed(share_rows(q), share_recv.at[q])
+        share_forward(q)
     for side in (0, 1):
 
         @pl.when(has[side])
         def _():
             landed(v_next.at[pl.ds(side * (ny + VDEEP), VDEEP)], v_next_recv.at[side])
 
-    def back_copy(j, q):
+    for side in (0, 1):
+
+        @pl.when(has[side])
+        def _():
+            halo_land(half, lone, 1 - side, half_recv)
+
+    def keep_result(y, x, combine):
+        for p, value in enumerate(combine(step_length / 2)):
+            result[p, y, pl.ds(x, 8)] = value
+
+    def send_back(q):
         rows = pl.ds(quarter * q, quarter)
-        return remote(
-            result.at[:, j, rows, there],
-            out_ref.at[:, own * gx + j, rows],
-            row_send, back_recv, {"gx": ox},
-        )
-
-    def stay_copy(j, q):
-        rows = pl.ds(quarter * q, quarter)
-        return pltpu.make_async_copy(result.at[:, j, rows, here], out_ref.at[:, own * gx + j, rows], stay_sem)
-
-    for j in range(own):
+        place = own * gx + lone
+        remote(result.at[:, rows, there], out_ref.at[:, place, rows], back_send, back_recv, {"gx": ox}).start()
+        pltpu.make_async_copy(result.at[:, rows, here], out_ref.at[:, place, rows], stay_sem).start()
+
+    exponential(half, v_next, lone, keep_result, send_back)
+    for n, (j, side_x) in enumerate(((shared, gx), (guest, ox))):
         for side in (0, 1):
 
             @pl.when(has[side])
             def _():
-                halo_land(half, j, 1 - side, half_recv)
-
-        def keep_result(y, x, combine):
+                if j == guest:
+                    landed(half.at[:, guest, pl.ds(halo_row(1 - side), DEEP), data], share_halo_recv.at[1 - side])
+                else:
+                    halo_land(half, j, 1 - side, half_recv)
+
+        def keep_local(y, x, combine):
             for p, value in enumerate(combine(step_length / 2)):
-                result[p, j, y, pl.ds(x, 8)] = value
-
-        def send_back(q):
-            back_copy(j, q).start()
-            stay_copy(j, q).start()
-
-        exponential(half, v_next, j, keep_result, send_back)
+                local_result[p, n, y, pl.ds(x, 8)] = value
+
+        exponential(half, v_next, j, keep_local, lambda i: None, only_here=True)
+        pltpu.make_async_copy(local_result.at[:, n], out_ref.at[:, own * side_x + shared], local_sem).start()
 
     pot_out.wait()
     sent(orb_v, row_send)
@@ -768,10 +840,13 @@
         @pl.when(has[d])
         def _():
             sent(v_next.at[pl.ds(0, VDEEP)], v_next_send.at[d])
-            sent(half.at[:, :, pl.ds(0, 2 * DEEP), pl.ds(edge, 2 * nx)], side_send.at[d])
-
-    pltpu.make_async_copy(result.at[..., here, :], out_ref.at[:, keep], stay_sem).wait()
-    landed(out_ref.at[:, give], back_recv)
+            sent(half.at[:, pl.ds(0, own), pl.ds(0, 2 * DEEP), data], side_send.at[d])
+            sent(half.at[:, guest, pl.ds(0, DEEP), data], share_side_send.at[d])
+
+    sent(orb_v.at[:, 0], back_send)
+    pltpu.make_async_copy(orb_v.at[:, 0], out_ref.at[:, 0], stay_sem).wait()
+    pltpu.make_async_copy(orb_v.at[:, pl.ds(0, own)], out_ref.at[:, pl.ds(0, own)], local_sem).wait()
+    landed(out_ref.at[:, own * ox + lone], back_recv)
 
 
 def leave(result, potential, result_out, potential_out, sems):
@@ -790,7 +865,7 @@
     own = nb // 2
     nq = ny // 4
     dma = pltpu.SemaphoreType.DMA
-    term = pltpu.VMEM((parts, own, ny + 2 * DEEP, 2 * nx + 16, nz), jnp.float32)
+    start, term = [pltpu.VMEM((parts, n, ny + 2 * DEEP, 2 * nx + 16, nz), jnp.float32) for n in (own, own + 1)]
     block = pltpu.VMEM((ny, nx, nz), jnp.float32)
     half_block = pltpu.VMEM((ny // 2, nx, nz), jnp.float32)
     wide = pltpu.VMEM((ny + 2 * VDEEP, 2 * nx, nz), jnp.float32)
@@ -803,7 +878,7 @@
         in_specs=[pl.BlockSpec(memory_space=pltpu.HBM)] * 2,
         out_specs=(pl.BlockSpec(memory_space=pl.ANY),) * 2,
         scratch_shapes=[
-            term, term, term, term, term,
+            start, term, term, term, term,
             pltpu.VMEM((parts, nb, ny, nx, nz), jnp.float32),
             pltpu.VMEM((ny, 2 * nx, nz), jnp.float32),
             wide, wide,
@@ -812,12 +887,14 @@
             block,
             pltpu.VMEM((3, ny, nx, nz), jnp.float32),
             block,
-            pltpu.VMEM((parts, own, ny, 2 * nx, nz), jnp.float32),
+            pltpu.VMEM((parts, ny, 2 * nx, nz), jnp.float32),
+            pltpu.VMEM((parts, 2, ny, nx, nz), jnp.float32),
             block,
             pltpu.VMEM((2 * nz, nz), jnp.bfloat16),
             dma((5,)), dma, dma, dma, dma((2,)), dma, dma((2,)), dma,
             dma((own, nq)), dma((2, own)), dma((2, own)), dma, dma, dma, dma, dma((2,)),
-            dma, dma((nq,)), dma((nq,)), dma((2,)), dma,
+            dma, dma((nq,)), dma((nq,)), dma((2,)), dma, dma, dma((nq,)), dma((2,)), dma((2,)),
+            dma,
             pltpu.SemaphoreType.REGULAR,
         ],
         compiler_params=pltpu.CompilerParams(

time: 31.2 us -> 29.5 us (0.946)
  Pallas kernels: 30.4 us -> 28.7 us
    pallas_call x1, Pallas kernels: 29.6 us -> 27.9 us  [whole_body(): pl.pallas_call(functools.partial(whole_kernel, counts), out_shape=(jax.Sh...]
where the time goes in v6:
time: 29.5 us; the launch traced here: 29.3 us
  Pallas kernels  28.7 us (97%)
  between operations  0.64 us (2%)
    pallas_call x1, Pallas kernels, whole_body(): pl.pallas_call(functools.partial(whole_kernel, counts), out_shape=(jax.Sh...  27.9 us
    pallas_call x1, Pallas kernels, whole_body(): pl.pallas_call(leave, out_shape=tuple((jax.ShapeDtypeStruct(a.shape, a.dt...  0.77 us

profile of v6, /device:TPU:0, one launch (start us, length us, event | category | flops | bytes accessed | tf_op | source)
XLA Modules:
  0.0 29.3 jit_solution(1620067616551486922)
XLA Ops:
  0.6 27.9 %shard_map.41 = (f32[2,4,12,8,128]{4,3,2,1,0:T(8,128)S(1)}, f32[12,8,128]{2,1,0:T(8,128)S(1)}) custom-call(f32[2,4,12,8,128]{4,3,2,1,0:T(8,128)} %bitcast.4, f32[12,8,128]{2,1,0:T(8,128)} %bitcast.5), custom_call_target="tpu_custom_call" | custom-call | tf_op jit(solution)/shard_map/pallas_call | solution.py:872
  28.6 0.8 %shard_map.42 = (f32[2,4,12,8,128]{4,3,2,1,0:T(8,128)}, f32[12,8,128]{2,1,0:T(8,128)}) custom-call(f32[2,4,12,8,128]{4,3,2,1,0:T(8,128)S(1)} %get-tuple-element.6.result, f32[12,8,128]{2,1,0:T(8,128)S(1)} %get-tuple-element.7.potential), custom_call_target="tpu_custom_call" | custom-call | tf_op jit(solution)/shard_map/pallas_call | solution.py:907
